TPU v7x, 32 devices: a whole 2x2x4 slice. The times are simulated.
32 devices in a mesh: dp: 4 (over x, core), expert: 4 (over z), etp: 2 (over y).
Axes of the slice: x: 2, y: 2, z: 4, core: 2. Of those that a mesh axis runs over, the one named last changes fastest.
Arguments:
- tokens: bfloat16 [4096, 3072], P(('dp', 'expert'), 'etp'), parts along dimension 0, may hold values from -6 to 6
- experts: int32 [4096, 2], P(('dp', 'expert')), parts along dimension 0, may hold values from 0 to 3, all different within a row; in each aligned block of 256 rows (0 to 255, 256 to 511, ...) at most 176 rows name the same one
- mixing: float32 [4096, 2], P(('dp', 'expert')), parts along dimension 0, may hold values from 0.2 to 1
- up_weight: bfloat16 [4, 3072, 8192], P('expert', None, 'etp'), may hold values from -0.109375 to 0.109375
- down_weight: bfloat16 [4, 8192, 3072], P('expert', 'etp'), may hold values from -0.0625 to 0.0625
Outputs:
- mixed: bfloat16 [4096, 3072], P(('dp', 'expert'), 'etp'), parts along dimension 0
There are 4 independent parts, one for each index of `dp`. A program takes and returns all parts, laid end to end along the dimension named above; an argument that names none is the same for every part. Nothing has to cross between parts.
Inputs may be any that keep to these rules, and one draw needn't show every extreme that they name: Each row names two different experts. In the rows of one index of expert (aligned blocks of 256 rows) no expert is named more than 176 times, a bound that some block reaches.
All inputs are finite; a program needn't handle non-finite values.
Results may differ from a plain program's by a relative error of at most 0.0078.
Values may be sent and summed in bfloat16 or wider, within the bound.
No kernel may reach another device: no remote copies, remote signals or barrier semaphores. Data moves between devices by JAX's collectives and lax.ppermute only.
A program may use at most 128 MiB of HBM per device.

v0:
```python
import jax
import jax.numpy as jnp
from jax import lax
from jax.sharding import PartitionSpec as P


def slot_table(chosen, expert_count, capacity):
    flat_ids = chosen.reshape(-1)
    one_hot = (flat_ids[:, None] == jnp.arange(expert_count, dtype=jnp.int32)[None, :]).astype(
        jnp.int32
    )
    before = jnp.cumsum(one_hot, axis=0) - one_hot
    position = jnp.sum(before * one_hot, axis=1)
    return (flat_ids * capacity + position).reshape(chosen.shape)


def dispatch_rows(block_tokens, slot_ids, slot_total):
    one_hot = (
        slot_ids[:, :, None] == jnp.arange(slot_total, dtype=jnp.int32)[None, None, :]
    ).astype(jnp.bfloat16)
    placing = jnp.sum(one_hot, axis=1)
    return jnp.einsum(
        "rs,rd->sd", placing, block_tokens, preferred_element_type=jnp.float32
    ).astype(jnp.bfloat16)


def local(tokens, experts, mixing, up_weight, down_weight):
    tok_rows = experts.shape[0]
    part_width = tokens.shape[1]
    expert_count = up_weight.shape[0] * lax.axis_size("expert")
    capacity = 2 * tok_rows // expert_count * 11 // 8
    slot_total = expert_count * capacity
    up_slab = up_weight[0]
    down_slab = down_weight[0]
    slot_ids = slot_table(experts, expert_count, capacity)
    outgoing = dispatch_rows(tokens, slot_ids, slot_total).reshape(
        expert_count, capacity, part_width
    )
    arrived = lax.all_to_all(outgoing, "expert", split_axis=0, concat_axis=0, tiled=True)
    gathered = lax.all_gather(arrived.reshape(slot_total, part_width), "etp", axis=1, tiled=True)
    up_proj = jnp.dot(gathered, up_slab, preferred_element_type=jnp.float32)
    hidden = jax.nn.silu(up_proj).astype(jnp.bfloat16)
    partial_sums = jnp.dot(hidden, down_slab, preferred_element_type=jnp.float32)
    own_cols = lax.psum_scatter(partial_sums, "etp", scatter_dimension=1, tiled=True).astype(
        jnp.bfloat16
    )
    outputs = lax.all_to_all(
        own_cols.reshape(expert_count, capacity, part_width),
        "expert",
        split_axis=0,
        concat_axis=0,
        tiled=True,
    )
    flat_out = outputs.reshape(slot_total, part_width)
    picked = (
        jnp.take(flat_out, slot_ids.reshape(-1), axis=0)
        .reshape(tok_rows, 2, part_width)
        .astype(jnp.float32)
    )
    mixed = jnp.sum(picked * mixing[:, :, None], axis=1)
    return mixed.astype(jnp.bfloat16)


def solution(mesh):
    placed = (
        P(("dp", "expert"), "etp"),
        P(("dp", "expert"), None),
        P(("dp", "expert"), None),
        P("expert", None, "etp"),
        P("expert", "etp", None),
    )
    return jax.shard_map(
        local, mesh=mesh, in_specs=placed, out_specs=P(("dp", "expert"), "etp"), check_vma=False
    )
```

profile of v0, /device:TPU:0, one launch (start us, length us, event | category | flops | bytes accessed | tf_op | source)
XLA Modules:
  0.0 352.5 jit_solution(7086791842899878181)
XLA Ops:
  6.5 0.0 copy-start
  6.5 0.0 all-gather.2.cloned.1.call-start
  6.5 0.9 copy.18
  7.4 0.1 eq.39
  7.6 0.1 reshape.81
  7.7 1.2 reduce-window.6
  9.0 0.2 slice_reduce_fusion
  9.2 0.2 reduce-window.9
  9.4 0.1 add_bitcast_fusion
  9.5 0.1 reduce_sum.35
  9.6 0.1 copy.20
  9.7 0.7 compare_and_fusion
  10.4 0.3 fusion.10
  10.7 0.0 copy-done
  10.7 0.7 convolution_convert_fusion
  11.4 55.9 %all_to_all.10 = bf16[4,176,1536]{2,1,0:T(8,128)(2,1)} all-to-all(bf16[4,176,1536]{2,1,0:T(8,128)(2,1)S(1)} %bitcast.47), channel_id=1, replica_groups=mesh['dp'=4,'expert'=4,'etp'=2] {'expert'}, dimensions={0} | all-to-all | bytes 4325376 | tf_op jit(solution)/shard_map/all_to_all | solution.py:39
  67.3 0.0 all-gather.2.cloned.1.call-update
  67.3 0.0 reduce-scatter.2.cloned.1.call-start
  67.4 57.5 %all-gather.2.cloned.1.call-done = bf16[704,3072]{1,0:T(8,128)(2,1)} async-done(((bf16[704,1536]{1,0:T(8,128)(2,1)}), bf16[704,3072]{1,0:T(8,128)(2,1)}) %all-gather.2.cloned.1.call-update) | async-done | bytes 4325392 | tf_op jit(solution)/shard_map/all_gather | solution.py:40
  124.9 23.9 %multiply_convert_fusion.4 = bf16[704,4096]{1,0:T(8,128)(2,1)S(1)} fusion(bf16[704,3072]{1,0:T(8,128)(2,1)} %all-gather.2.cloned.1.call-done, bf16[1,3072,4096]{2,1,0:T(8,128)(2,1)} %param.8), kind=kOutput, calls=%fused_computation.5.clone.clone.1 | convolution fusion | flops 17731158016 | bytes 35258368 | tf_op jit(solution)/shard_map/dot_general | solution.py:41
  148.8 22.8 %fusion = f32[704,3072]{1,0:T(8,128)} fusion(bf16[1,4096,3072]{2,1,0:T(8,128)(2,1)} %param.9, bf16[704,4096]{1,0:T(8,128)(2,1)S(1)} %multiply_convert_fusion.4), kind=kOutput, calls=%fused_computation.1 | convolution fusion | flops 17716740096 | bytes 39583744 | tf_op jit(solution)/shard_map/dot_general | solution.py:43
  171.6 0.0 reduce-scatter.2.cloned.1.call-update
  171.6 0.0 copy-start.2
  171.6 0.0 copy-start.3
  171.6 102.3 %reduce-scatter.2.cloned.1.call-done = f32[704,1536]{1,0:T(8,128)} async-done(((f32[704,3072]{1,0:T(8,128)}), f32[704,1536]{1,0:T(8,128)}) %reduce-scatter.2.cloned.1.call-update) | async-done | bytes 4325392 | tf_op jit(solution)/shard_map/reduce_scatter | solution.py:44
  273.9 3.8 %convert_element_type.32 = bf16[704,1536]{1,0:T(8,128)(2,1)} convert(f32[704,1536]{1,0:T(8,128)} %reduce-scatter.2.cloned.1.call-done) | non-fusion elementwise | flops 1081344 | bytes 6488064 | tf_op jit(solution)/shard_map/convert_element_type | solution.py:44
  277.7 4.6 %all-to-all-start.1 = ((bf16[4,176,1536]{2,1,0:T(8,128)(2,1)}), bf16[4,176,1536]{2,1,0:T(8,128)(2,1)S(1)}, u32[]{:S(2)}, u32[]{:S(2)}) async-start(bf16[4,176,1536]{2,1,0:T(8,128)(2,1)} %bitcast.48), calls=%async_computation.2 | async-start | bytes 4325376 | tf_op jit(solution)/shard_map/all_to_all | solution.py:47
  282.4 0.0 copy-done.2
  282.4 0.1 copy.22
  282.5 0.1 mul.40
  282.7 0.2 copy.21
  282.8 0.0 copy-done.3
  282.9 0.1 copy.23
  283.0 48.8 %all-to-all-done.1 = bf16[4,176,1536]{2,1,0:T(8,128)(2,1)S(1)} async-done(((bf16[4,176,1536]{2,1,0:T(8,128)(2,1)}), bf16[4,176,1536]{2,1,0:T(8,128)(2,1)S(1)}, u32[]{:S(2)}, u32[]{:S(2)}) %all-to-all-start.1) | async-done | bytes 2162720 | tf_op jit(solution)/shard_map/all_to_all | solution.py:47
  331.8 0.0 copy-start.1
  331.8 3.0 gather_fusion
  334.8 3.5 gather.7
  338.3 7.4 %multiply_reduce_fusion = bf16[256,1536]{1,0:T(8,128)(2,1)} fusion(bf16[256,2,1536]{2,1,0:T(2,128)(2,1)S(1)} %gather.7, pred[256,2]{1,0:T(8,128)(4,1)S(1)} %copy.21, f32[256,2]{1,0:T(8,128)S(1)} %copy.23), kind=kLoop, calls=%fused_computation.8 | loop fusion | flops 2752512 | bytes 2361856 | tf_op jit(solution)/shard_map/reduce_sum | solution.py:60
  345.7 0.0 copy-done.1
  (5 shorter events, 0.0 us)
Async XLA Ops:
  6.5 4.2 %copy-start = (bf16[256,1536]{1,0:T(8,128)(2,1)S(1)}, bf16[256,1536]{1,0:T(8,128)(2,1)}, u32[]{:S(2)}) copy-start(bf16[256,1536]{1,0:T(8,128)(2,1)} %param.5) | copy-start | bytes 2359300
  6.5 118.4 %all-gather.2.cloned.1.call-start = ((), (), s32[]{:S(2)}) async-start(), calls=%async_computation.3 | async-start | bytes 6488064 | tf_op jit(solution)/shard_map/all_gather | solution.py:40
  67.3 206.6 %reduce-scatter.2.cloned.1.call-start = ((), (), s32[]{:S(2)}) async-start(), calls=%async_computation.4 | async-start | bytes 12976128 | tf_op jit(solution)/shard_map/reduce_scatter | solution.py:44
  171.6 110.7 %copy-start.2 = (s32[256,2]{0,1:T(2,128)S(1)}, s32[256,2]{0,1:T(2,128)}, u32[]{:S(2)}) copy-start(s32[256,2]{0,1:T(2,128)} %param.6) | copy-start | bytes 6148
  171.6 111.2 %copy-start.3 = (f32[256,2]{0,1:T(2,128)S(1)}, f32[256,2]{0,1:T(2,128)}, u32[]{:S(2)}) copy-start(f32[256,2]{0,1:T(2,128)} %param.7) | copy-start | bytes 6148
  277.7 54.1 %all-to-all-start.1 = ((bf16[4,176,1536]{2,1,0:T(8,128)(2,1)}), bf16[4,176,1536]{2,1,0:T(8,128)(2,1)S(1)}, u32[]{:S(2)}, u32[]{:S(2)}) async-start(bf16[4,176,1536]{2,1,0:T(8,128)(2,1)} %bitcast.48), calls=%async_computation.2 | async-start | bytes 4325376 | tf_op jit(solution)/shard_map/all_to_all | solution.py:47
  331.8 13.9 %copy-start.1 = (bf16[256,1536]{1,0:T(8,128)(2,1)S(1)}, bf16[256,1536]{1,0:T(8,128)(2,1)}, u32[]{:S(2)}) copy-start(bf16[256,1536]{1,0:T(8,128)(2,1)} %param.5) | copy-start | bytes 2359300
Sparse Core Ops, SparseCore 0:
  67.4 57.4 all-gather.1
  171.7 102.1 reduce-scatter.1
where the time goes:
time: 353 us
  waiting for transfers between devices  209 us (59%)
  blocking collectives  55.9 us (16%)
  matrix products  47.4 us (13%)
  other arithmetic  13.8 us (4%)
  between operations  13.5 us (4%)
  local copies, waits for them, and re-layouts  8.66 us (2%)
  starting transfers between devices  4.67 us (1%)
    reduce_scatter x1, waiting for transfers between devices, local(): lax.psum_scatter(partial_sums, 'etp', scatter_dimension=1, tiled=True)  102 us
    all_gather x1, waiting for transfers between devices, local(): lax.all_gather(arrived.reshape(slot_total, part_width), 'etp', axis=1, ti...  57.5 us
    all_to_all x1, blocking collectives, local(): lax.all_to_all(outgoing, 'expert', split_axis=0, concat_axis=0, tiled=True)  55.9 us
    all_to_all x1, waiting for transfers between devices, local(): lax.all_to_all(own_cols.reshape(expert_count, capacity, part_width), 'exp...  48.8 us
    dot_general x1, matrix products, local(): up_proj = jnp.dot(gathered, up_slab, preferred_element_type=jnp.float32)  23.9 us
    dot_general x1, matrix products, local(): jnp.dot(hidden, down_slab, preferred_element_type=jnp.float32)  22.8 us
    reduce_sum x1, other arithmetic, local(): mixed = jnp.sum(picked * mixing[:, :, None], axis=1)  7.44 us
  transfers between devices with their start and end apart: 3, of which 3 were waited for; matrix products, arithmetic and copies ran while one was open for 0% of the time, Pallas kernels for 0%

commit v1 on v0

v1 whole, which is shorter than its diff:
```python
import jax
import jax.numpy as jnp
from jax import lax
from jax.sharding import PartitionSpec as P


def positions(chosen, expert_count):
    flat_ids = chosen.reshape(-1)
    one_hot = (flat_ids[:, None] == jnp.arange(expert_count, dtype=jnp.int32)[None, :]).astype(
        jnp.int32
    )
    before = jnp.cumsum(one_hot, axis=0) - one_hot
    return jnp.sum(before * one_hot, axis=1).reshape(chosen.shape)


def one_hot_rows(slot_ids, slot_total):
    return (
        slot_ids[:, :, None] == jnp.arange(slot_total, dtype=jnp.int32)[None, None, :]
    ).astype(jnp.bfloat16)


def local(tokens, experts, mixing, up_weight, down_weight):
    tok_rows = experts.shape[0]
    width = tokens.shape[1]
    groups = lax.axis_size("expert")
    halves = lax.axis_size("etp")
    capacity = 2 * tok_rows // groups * 11 // 8
    slot_total = groups * capacity
    up_slab = up_weight[0]
    down_slab = down_weight[0]
    me = lax.axis_index("expert")
    part = lax.axis_index("etp")

    def partner(offset):
        return [(i, i ^ offset) for i in range(groups)]

    def across(rows, offset):
        return rows if offset == 0 else lax.ppermute(rows, "expert", partner(offset))

    def join(rows):
        if halves != 2:
            return lax.all_gather(rows, "etp", axis=1, tiled=True)
        other = lax.ppermute(rows, "etp", [(0, 1), (1, 0)])
        first = jnp.where(part == 0, rows, other)
        second = jnp.where(part == 0, other, rows)
        return jnp.concatenate([first, second], axis=1)

    def reduce(sums):
        if halves != 2:
            return lax.psum_scatter(sums, "etp", scatter_dimension=1, tiled=True).astype(
                jnp.bfloat16
            )
        first, second = sums[:, :width], sums[:, width:]
        keep = jnp.where(part == 0, first, second)
        send = jnp.where(part == 0, second, first).astype(jnp.bfloat16)
        other = lax.ppermute(send, "etp", [(0, 1), (1, 0)])
        return (keep + other.astype(jnp.float32)).astype(jnp.bfloat16)

    slot_ids = (experts ^ me) * capacity + positions(experts, groups)
    placing = one_hot_rows(slot_ids, slot_total)
    outgoing = jnp.einsum(
        "rs,rd->sd", jnp.sum(placing, axis=1), tokens, preferred_element_type=jnp.float32
    ).astype(jnp.bfloat16)
    order = sorted(range(groups), key=lambda k: (k != 0, -(k & -k), k))
    returned = {}
    for offset in order:
        rows = across(outgoing[offset * capacity : (offset + 1) * capacity], offset)
        gathered = join(rows)
        up_proj = jnp.dot(gathered, up_slab, preferred_element_type=jnp.float32)
        hidden = jax.nn.silu(up_proj).astype(jnp.bfloat16)
        sums = jnp.dot(hidden, down_slab, preferred_element_type=jnp.float32)
        returned[offset] = across(reduce(sums), offset)
    mixed = jnp.zeros((tok_rows, width), jnp.float32)
    for offset in order:
        cols = placing[:, :, offset * capacity : (offset + 1) * capacity]
        for k in range(2):
            mixed = mixed + mixing[:, k : k + 1] * jnp.dot(
                cols[:, k], returned[offset], preferred_element_type=jnp.float32
            )
    return mixed.astype(jnp.bfloat16)


def solution(mesh):
    placed = (
        P(("dp", "expert"), "etp"),
        P(("dp", "expert"), None),
        P(("dp", "expert"), None),
        P("expert", None, "etp"),
        P("expert", "etp", None),
    )
    return jax.shard_map(
        local, mesh=mesh, in_specs=placed, out_specs=P(("dp", "expert"), "etp"), check_vma=False
    )
```

time: 353 us -> 223 us (0.63)
  waiting for transfers between devices: 209 us -> 91.2 us
  blocking collectives: 55.9 us -> 0 us
  matrix products: 47.4 us -> 88.3 us
  starting transfers between devices: 4.67 us -> 21.8 us
  between operations: 13.5 us -> 0.23 us
  local copies, waits for them, and re-layouts: 8.66 us -> 1.66 us
  other arithmetic: 13.8 us -> 19.2 us
    reduce_scatter x1 -> x0, waiting for transfers between devices: 102 us -> none  [local(): lax.psum_scatter(partial_sums, 'etp', scatter_dimension=1, tiled=True)]
    ppermute x0 -> x14, waiting for transfers between devices: none -> 91.2 us  [the longest x6 56.2 us: across(): lax.ppermute(rows, 'expert', partner(offset))]
    all_gather x1 -> x0, waiting for transfers between devices: 57.5 us -> none  [local(): lax.all_gather(arrived.reshape(slot_total, part_width), 'etp', axis=1, ti...]
    all_to_all x1 -> x0, blocking collectives: 55.9 us -> none  [local(): lax.all_to_all(outgoing, 'expert', split_axis=0, concat_axis=0, tiled=True)]
    all_to_all x1 -> x0, waiting for transfers between devices: 48.8 us -> none  [local(): lax.all_to_all(own_cols.reshape(expert_count, capacity, part_width), 'exp...]
    dot_general x3 -> x13, matrix products: 47.4 us -> 88.3 us  [the longest x4 82.9 us: local(): sums = jnp.dot(hidden, down_slab, preferred_element_type=jnp.float32)]
    ppermute x0 -> x14, starting transfers between devices: none -> 21.8 us  [the longest x6 9.59 us: across(): lax.ppermute(rows, 'expert', partner(offset))]
    select_n x1 -> x4, other arithmetic: 0.01 us -> 7.7 us  [join(): first = jnp.where(part == 0, rows, other)]
  transfers between devices with their start and end apart: 3 -> 14, of which waited for: 3 -> 8; matrix products, arithmetic and copies ran while one was open for 0% -> 45% of each run, Pallas kernels for 0% -> 0%
where the time goes in v1:
time: 223 us; the launch traced here: 222 us
  waiting for transfers between devices  91.2 us (41%)
  matrix products  88.3 us (40%)
  starting transfers between devices  21.8 us (10%)
  other arithmetic  19.2 us (9%)
    dot_general x4, matrix products, local(): sums = jnp.dot(hidden, down_slab, preferred_element_type=jnp.float32)  82.9 us
    ppermute x6, waiting for transfers between devices, across(): lax.ppermute(rows, 'expert', partner(offset))  56.2 us
    ppermute x4, waiting for transfers between devices, join(): other = lax.ppermute(rows, 'etp', [(0, 1), (1, 0)])  32.3 us
    ppermute x6, starting transfers between devices, across(): lax.ppermute(rows, 'expert', partner(offset))  9.59 us
    select_n x4, other arithmetic, join(): first = jnp.where(part == 0, rows, other)  7.7 us
    ppermute x4, starting transfers between devices, join(): other = lax.ppermute(rows, 'etp', [(0, 1), (1, 0)])  6.66 us
    ppermute x4, starting transfers between devices, reduce(): other = lax.ppermute(send, 'etp', [(0, 1), (1, 0)])  5.54 us
    convert_element_type x4, other arithmetic, reduce(): send = jnp.where(part == 0, second, first).astype(jnp.bfloat16)  5.07 us
  transfers between devices with their start and end apart: 14, of which 8 were waited for; matrix products, arithmetic and copies ran while one was open for 45% of the time, Pallas kernels for 0%

profile of v1, /device:TPU:0, one launch (start us, length us, event | category | flops | bytes accessed | tf_op | source)
XLA Modules:
  0.0 222.4 jit_solution(7723889623027234474)
XLA Ops:
  0.0 0.9 copy.15
  0.9 0.1 eq.60
  1.0 0.1 eq.26
  1.2 1.2 reduce-window.6
  2.4 0.2 slice_reduce_fusion
  2.6 0.2 reduce-window.9
  2.8 0.1 add_bitcast_fusion
  2.9 0.1 reshape.22
  3.1 0.1 copy.17
  3.2 0.7 multiply_add_fusion
  3.9 0.3 convert_reduce_fusion
  4.2 0.7 convolution_convert_fusion
  4.9 3.1 %collective-permute-start = (bf16[176,1536]{1,0:T(8,128)(2,1)S(1)}, bf16[176,1536]{1,0:T(8,128)(2,1)}, u32[]{:S(2)}, u32[]{:S(2)}) collective-permute-start(bf16[176,1536]{1,0:T(8,128)(2,1)S(1)} %slice.116), channel_id=1, source_target_pairs={{0,1},{1,0},{2,3},{3,2},{4,5},{5,4},{6,7},{7,6},{8,9},{9,8},{10,11... | collective-permute-start | bytes 1622024 | tf_op jit(solution)/shard_map/ppermute | solution.py:43
  8.0 12.4 %collective-permute-done = bf16[176,1536]{1,0:T(8,128)(2,1)} collective-permute-done((bf16[176,1536]{1,0:T(8,128)(2,1)S(1)}, bf16[176,1536]{1,0:T(8,128)(2,1)}, u32[]{:S(2)}, u32[]{:S(2)}) %collective-permute-start) | collective-permute-done | bytes 540704 | tf_op jit(solution)/shard_map/ppermute | solution.py:43
  20.4 2.2 %broadcast_select_fusion.7 = (bf16[176,1536]{1,0:T(8,128)(2,1)S(1)}, bf16[176,1536]{1,0:T(8,128)(2,1)S(1)}, bf16[176,1536]{1,0:T(8,128)(2,1)}, bf16[176,1536]{1,0:T(8,128)(2,1)}, bf16[176,1536]{1,0:T(8,128)(2,1)}) fusion(bf16[176,1536]{1,0:T(8,128)(2,1)} %collective-permute-done, pred[]{:T(512)S(6)} %eq.67, bf16[704,1536]{1,0:T(8,128)(2,1)S(1)} %convolution_convert_fusion), kind=kLoop, calls=%fused_computation.70 | loop fusion | flops 540672 | bytes 5406721 | tf_op jit(solution)/shard_map/jit(_where)/select_n | solution.py:44
  22.6 3.8 %collective-permute-start.10 = (bf16[176,1536]{1,0:T(8,128)(2,1)}, bf16[176,1536]{1,0:T(8,128)(2,1)}, u32[]{:S(2)}, u32[]{:S(2)}) collective-permute-start(bf16[176,1536]{1,0:T(8,128)(2,1)} %get-tuple-element.7), channel_id=1, source_target_pairs={{0,6},{2,4},{4,2},{6,0},{1,7},{3,5},{5,3},{7,1},{8,14},{10,12},{12... | collective-permute-start | bytes 1622024 | tf_op jit(solution)/shard_map/ppermute | solution.py:38
  26.4 0.0 collective-permute-start.6
  26.4 0.6 collective-permute-start.2
  27.0 20.0 %fusion.6 = f32[176,3072]{1,0:T(8,128)S(1)} fusion(bf16[1,4096,3072]{2,1,0:T(8,128)(2,1)} %param.9, bf16[1,3072,4096]{2,1,0:T(8,128)(2,1)} %param.8, bf16[176,1536]{1,0:T(8,128)(2,1)S(1)} %get-tuple-element.6, bf16[176,1536]{1,0:T(8,128)(2,1)S(1)} %get-tuple-element.5), kind=kOutput, calls=%fused_computation.6 | convolution fusion | flops 8864137216 | bytes 53575680 | tf_op jit(solution)/shard_map/dot_general | solution.py:71
  47.0 0.0 copy-start.4
  47.1 0.1 select_convert_fusion.3
  47.2 1.8 collective-permute-start.1
  49.0 0.2 iota_compare_fusion
  49.2 0.0 collective-permute-done.10
  49.2 0.6 collective-permute-start.11
  49.8 1.2 collective-permute-done.6
  51.0 1.5 collective-permute-start.7
  52.5 19.6 %collective-permute-done.2 = bf16[176,1536]{1,0:T(8,128)(2,1)} collective-permute-done((bf16[176,1536]{1,0:T(8,128)(2,1)}, bf16[176,1536]{1,0:T(8,128)(2,1)}, u32[]{:S(2)}, u32[]{:S(2)}) %collective-permute-start.2) | collective-permute-done | bytes 540704 | tf_op jit(solution)/shard_map/ppermute | solution.py:38
  72.1 1.5 collective-permute-start.3
  73.6 0.0 collective-permute-done.1
  73.6 0.2 add_convert_fusion.3
  73.8 0.4 convolution_multiply_fusion.6
  74.3 0.4 fusion.38
  74.7 19.9 %collective-permute-done.3 = bf16[176,1536]{1,0:T(8,128)(2,1)S(1)} collective-permute-done((bf16[176,1536]{1,0:T(8,128)(2,1)}, bf16[176,1536]{1,0:T(8,128)(2,1)S(1)}, u32[]{:S(2)}, u32[]{:S(2)}) %collective-permute-start.3) | collective-permute-done | bytes 540704 | tf_op jit(solution)/shard_map/ppermute | solution.py:43
  94.6 1.1 broadcast_select_fusion.5
  95.7 21.4 %fusion.4 = f32[176,3072]{1,0:T(8,128)} fusion(bf16[1,4096,3072]{2,1,0:T(8,128)(2,1)} %param.9, bf16[1,3072,4096]{2,1,0:T(8,128)(2,1)} %param.8, bf16[176,1536]{1,0:T(8,128)(2,1)S(1)} %get-tuple-element.11, bf16[176,1536]{1,0:T(8,128)(2,1)S(1)} %get-tuple-element.10), kind=kOutput, calls=%fused_computation.4 | convolution fusion | flops 8864137216 | bytes 53575680 | tf_op jit(solution)/shard_map/dot_general | solution.py:71
  117.1 1.7 select_convert_fusion.2
  118.7 1.6 collective-permute-start.4
  120.3 0.0 collective-permute-done.11
  120.3 2.1 broadcast_select_fusion.1
  122.4 20.7 %fusion = f32[176,3072]{1,0:T(8,128)} fusion(bf16[1,4096,3072]{2,1,0:T(8,128)(2,1)} %param.9, bf16[1,3072,4096]{2,1,0:T(8,128)(2,1)} %param.8, bf16[176,1536]{1,0:T(8,128)(2,1)} %get-tuple-element.15, bf16[176,1536]{1,0:T(8,128)(2,1)S(1)} %get-tuple-element.14), kind=kOutput, calls=%fused_computation | convolution fusion | flops 8864137216 | bytes 53575680 | tf_op jit(solution)/shard_map/dot_general | solution.py:71
  143.1 1.7 select_convert_fusion
  144.8 0.6 collective-permute-start.12
  145.3 2.3 %broadcast_select_fusion.3 = (bf16[176,1536]{1,0:T(8,128)(2,1)}, bf16[176,1536]{1,0:T(8,128)(2,1)}) fusion(bf16[176,1536]{1,0:T(8,128)(2,1)} %collective-permute-done.6, bf16[176,1536]{1,0:T(8,128)(2,1)} %collective-permute-done.7, pred[]{:T(512)S(6)} %eq.67), kind=kLoop, calls=%fused_computation.66 | loop fusion | flops 540672 | bytes 2162689 | tf_op jit(solution)/shard_map/jit(_where)/select_n | solution.py:44
  147.6 20.8 %fusion.2 = f32[176,3072]{1,0:T(8,128)} fusion(bf16[1,4096,3072]{2,1,0:T(8,128)(2,1)} %param.9, bf16[1,3072,4096]{2,1,0:T(8,128)(2,1)} %param.8, bf16[176,1536]{1,0:T(8,128)(2,1)} %get-tuple-element.13, bf16[176,1536]{1,0:T(8,128)(2,1)} %get-tuple-element.12), kind=kOutput, calls=%fused_computation.2 | convolution fusion | flops 8864137216 | bytes 53575680 | tf_op jit(solution)/shard_map/dot_general | solution.py:71
  168.4 1.7 select_convert_fusion.1
  170.1 1.6 collective-permute-start.8
  171.7 1.9 add_convert_fusion
  173.6 3.6 %collective-permute-start.13 = (bf16[176,1536]{1,0:T(8,128)(2,1)S(1)}, bf16[176,1536]{1,0:T(8,128)(2,1)S(1)}, u32[]{:S(2)}, u32[]{:S(2)}) collective-permute-start(bf16[176,1536]{1,0:T(8,128)(2,1)S(1)} %add_convert_fusion), channel_id=1, source_target_pairs={{0,6},{2,4},{4,2},{6,0},{1,7},{3,5},{5,3},{7,1},{8,14},{10,12},{12... | collective-permute-start | bytes 1622024 | tf_op jit(solution)/shard_map/ppermute | solution.py:38
  177.3 1.3 add_convert_fusion.2
  178.6 0.1 collective-permute-start.5
  178.6 2.7 %collective-permute-done.8 = bf16[176,1536]{1,0:T(8,128)(2,1)S(1)} collective-permute-done((bf16[176,1536]{1,0:T(8,128)(2,1)S(1)}, bf16[176,1536]{1,0:T(8,128)(2,1)S(1)}, u32[]{:S(2)}, u32[]{:S(2)}) %collective-permute-start.8) | collective-permute-done | bytes 540704 | tf_op jit(solution)/shard_map/ppermute | solution.py:56
  181.4 0.2 add_convert_fusion.1
  181.6 1.5 collective-permute-start.9
  183.1 7.6 %collective-permute-done.13 = bf16[176,1536]{1,0:T(8,128)(2,1)S(1)} collective-permute-done((bf16[176,1536]{1,0:T(8,128)(2,1)S(1)}, bf16[176,1536]{1,0:T(8,128)(2,1)S(1)}, u32[]{:S(2)}, u32[]{:S(2)}) %collective-permute-start.13) | collective-permute-done | bytes 540704 | tf_op jit(solution)/shard_map/ppermute | solution.py:38
  190.7 0.4 convolution_multiply_fusion
  191.1 0.4 convolution_multiply_fusion.1
  191.6 17.1 %collective-permute-done.9 = bf16[176,1536]{1,0:T(8,128)(2,1)S(1)} collective-permute-done((bf16[176,1536]{1,0:T(8,128)(2,1)S(1)}, bf16[176,1536]{1,0:T(8,128)(2,1)S(1)}, u32[]{:S(2)}, u32[]{:S(2)}) %collective-permute-start.9) | collective-permute-done | bytes 540704 | tf_op jit(solution)/shard_map/ppermute | solution.py:38
  208.7 0.4 convolution_multiply_fusion.2
  209.1 0.4 convolution_multiply_fusion.3
  209.5 10.7 %collective-permute-done.5 = bf16[176,1536]{1,0:T(8,128)(2,1)S(1)} collective-permute-done((bf16[176,1536]{1,0:T(8,128)(2,1)S(1)}, bf16[176,1536]{1,0:T(8,128)(2,1)S(1)}, u32[]{:S(2)}, u32[]{:S(2)}) %collective-permute-start.5) | collective-permute-done | bytes 540704 | tf_op jit(solution)/shard_map/ppermute | solution.py:38
  220.3 0.4 convolution_multiply_fusion.4
  220.7 0.0 copy-start.1
  220.7 1.7 fusion.39
  (15 shorter events, 0.1 us)
Async XLA Ops:
  0.0 4.1 %copy-start = (bf16[256,1536]{1,0:T(8,128)(2,1)S(1)}, bf16[256,1536]{1,0:T(8,128)(2,1)}, u32[]{:S(2)}) copy-start(bf16[256,1536]{1,0:T(8,128)(2,1)} %param.5) | copy-start | bytes 2359300
  4.9 15.4 %collective-permute-start = (bf16[176,1536]{1,0:T(8,128)(2,1)S(1)}, bf16[176,1536]{1,0:T(8,128)(2,1)}, u32[]{:S(2)}, u32[]{:S(2)}) collective-permute-start(bf16[176,1536]{1,0:T(8,128)(2,1)S(1)} %slice.116), channel_id=1, source_target_pairs={{0,1},{1,0},{2,3},{3,2},{4,5},{5,4},{6,7},{7,6},{8,9},{9,8},{10,11... | collective-permute-start | bytes 1622024 | tf_op jit(solution)/shard_map/ppermute | solution.py:43
  22.6 26.6 %collective-permute-start.10 = (bf16[176,1536]{1,0:T(8,128)(2,1)}, bf16[176,1536]{1,0:T(8,128)(2,1)}, u32[]{:S(2)}, u32[]{:S(2)}) collective-permute-start(bf16[176,1536]{1,0:T(8,128)(2,1)} %get-tuple-element.7), channel_id=1, source_target_pairs={{0,6},{2,4},{4,2},{6,0},{1,7},{3,5},{5,3},{7,1},{8,14},{10,12},{12... | collective-permute-start | bytes 1622024 | tf_op jit(solution)/shard_map/ppermute | solution.py:38
  26.4 24.6 %collective-permute-start.6 = (bf16[176,1536]{1,0:T(8,128)(2,1)}, bf16[176,1536]{1,0:T(8,128)(2,1)}, u32[]{:S(2)}, u32[]{:S(2)}) collective-permute-start(bf16[176,1536]{1,0:T(8,128)(2,1)} %get-tuple-element.8), channel_id=1, source_target_pairs={{0,2},{2,0},{4,6},{6,4},{1,3},{3,1},{5,7},{7,5},{8,10},{10,8},{12,... | collective-permute-start | bytes 1622024 | tf_op jit(solution)/shard_map/ppermute | solution.py:38
  26.4 45.6 %collective-permute-start.2 = (bf16[176,1536]{1,0:T(8,128)(2,1)}, bf16[176,1536]{1,0:T(8,128)(2,1)}, u32[]{:S(2)}, u32[]{:S(2)}) collective-permute-start(bf16[176,1536]{1,0:T(8,128)(2,1)} %get-tuple-element.9), channel_id=1, source_target_pairs={{0,4},{2,6},{4,0},{6,2},{1,5},{3,7},{5,1},{7,3},{8,12},{10,14},{12... | collective-permute-start | bytes 1622024 | tf_op jit(solution)/shard_map/ppermute | solution.py:38
  47.0 1.9 copy-start.4
  47.2 26.4 %collective-permute-start.1 = (bf16[176,1536]{1,0:T(8,128)(2,1)S(1)}, bf16[176,1536]{1,0:T(8,128)(2,1)S(1)}, u32[]{:S(2)}, u32[]{:S(2)}) collective-permute-start(bf16[176,1536]{1,0:T(8,128)(2,1)S(1)} %select_convert_fusion.3), channel_id=1, source_target_pairs={{0,1},{1,0},{2,3},{3,2},{4,5},{5,4},{6,7},{7,6},{8,9},{9,8},{10,11... | collective-permute-start | bytes 1622024 | tf_op jit(solution)/shard_map/ppermute | solution.py:56
  49.2 71.1 %collective-permute-start.11 = (bf16[176,1536]{1,0:T(8,128)(2,1)}, bf16[176,1536]{1,0:T(8,128)(2,1)}, u32[]{:S(2)}, u32[]{:S(2)}) collective-permute-start(bf16[176,1536]{1,0:T(8,128)(2,1)} %collective-permute-done.10), channel_id=1, source_target_pairs={{0,1},{1,0},{2,3},{3,2},{4,5},{5,4},{6,7},{7,6},{8,9},{9,8},{10,11... | collective-permute-start | bytes 1622024 | tf_op jit(solution)/shard_map/ppermute | solution.py:43
  51.0 94.3 %collective-permute-start.7 = (bf16[176,1536]{1,0:T(8,128)(2,1)}, bf16[176,1536]{1,0:T(8,128)(2,1)}, u32[]{:S(2)}, u32[]{:S(2)}) collective-permute-start(bf16[176,1536]{1,0:T(8,128)(2,1)} %collective-permute-done.6), channel_id=1, source_target_pairs={{0,1},{1,0},{2,3},{3,2},{4,5},{5,4},{6,7},{7,6},{8,9},{9,8},{10,11... | collective-permute-start | bytes 1622024 | tf_op jit(solution)/shard_map/ppermute | solution.py:43
  72.1 22.5 %collective-permute-start.3 = (bf16[176,1536]{1,0:T(8,128)(2,1)}, bf16[176,1536]{1,0:T(8,128)(2,1)S(1)}, u32[]{:S(2)}, u32[]{:S(2)}) collective-permute-start(bf16[176,1536]{1,0:T(8,128)(2,1)} %collective-permute-done.2), channel_id=1, source_target_pairs={{0,1},{1,0},{2,3},{3,2},{4,5},{5,4},{6,7},{7,6},{8,9},{9,8},{10,11... | collective-permute-start | bytes 1622024 | tf_op jit(solution)/shard_map/ppermute | solution.py:43
  118.7 58.5 %collective-permute-start.4 = (bf16[176,1536]{1,0:T(8,128)(2,1)S(1)}, bf16[176,1536]{1,0:T(8,128)(2,1)}, u32[]{:S(2)}, u32[]{:S(2)}) collective-permute-start(bf16[176,1536]{1,0:T(8,128)(2,1)S(1)} %select_convert_fusion.2), channel_id=1, source_target_pairs={{0,1},{1,0},{2,3},{3,2},{4,5},{5,4},{6,7},{7,6},{8,9},{9,8},{10,11... | collective-permute-start | bytes 1622024 | tf_op jit(solution)/shard_map/ppermute | solution.py:56
  144.8 26.9 %collective-permute-start.12 = (bf16[176,1536]{1,0:T(8,128)(2,1)S(1)}, bf16[176,1536]{1,0:T(8,128)(2,1)}, u32[]{:S(2)}, u32[]{:S(2)}) collective-permute-start(bf16[176,1536]{1,0:T(8,128)(2,1)S(1)} %select_convert_fusion), channel_id=1, source_target_pairs={{0,1},{1,0},{2,3},{3,2},{4,5},{5,4},{6,7},{7,6},{8,9},{9,8},{10,11... | collective-permute-start | bytes 1622024 | tf_op jit(solution)/shard_map/ppermute | solution.py:56
  170.1 7.2 %copy-start.2 = (f32[176,3072]{1,0:T(8,128)S(1)}, f32[176,3072]{1,0:T(8,128)}, u32[]{:S(2)}) copy-start(f32[176,3072]{1,0:T(8,128)} %fusion.4) | copy-start | bytes 6488068
  170.1 11.2 %collective-permute-start.8 = (bf16[176,1536]{1,0:T(8,128)(2,1)S(1)}, bf16[176,1536]{1,0:T(8,128)(2,1)S(1)}, u32[]{:S(2)}, u32[]{:S(2)}) collective-permute-start(bf16[176,1536]{1,0:T(8,128)(2,1)S(1)} %select_convert_fusion.1), channel_id=1, source_target_pairs={{0,1},{1,0},{2,3},{3,2},{4,5},{5,4},{6,7},{7,6},{8,9},{9,8},{10,11... | collective-permute-start | bytes 1622024 | tf_op jit(solution)/shard_map/ppermute | solution.py:56
  173.6 7.7 %copy-start.3 = (f32[176,3072]{1,0:T(8,128)S(1)}, f32[176,3072]{1,0:T(8,128)}, u32[]{:S(2)}) copy-start(f32[176,3072]{1,0:T(8,128)} %fusion.2) | copy-start | bytes 6488068
  173.6 17.1 %collective-permute-start.13 = (bf16[176,1536]{1,0:T(8,128)(2,1)S(1)}, bf16[176,1536]{1,0:T(8,128)(2,1)S(1)}, u32[]{:S(2)}, u32[]{:S(2)}) collective-permute-start(bf16[176,1536]{1,0:T(8,128)(2,1)S(1)} %add_convert_fusion), channel_id=1, source_target_pairs={{0,6},{2,4},{4,2},{6,0},{1,7},{3,5},{5,3},{7,1},{8,14},{10,12},{12... | collective-permute-start | bytes 1622024 | tf_op jit(solution)/shard_map/ppermute | solution.py:38
  178.6 41.7 %collective-permute-start.5 = (bf16[176,1536]{1,0:T(8,128)(2,1)S(1)}, bf16[176,1536]{1,0:T(8,128)(2,1)S(1)}, u32[]{:S(2)}, u32[]{:S(2)}) collective-permute-start(bf16[176,1536]{1,0:T(8,128)(2,1)S(1)} %add_convert_fusion.2), channel_id=1, source_target_pairs={{0,4},{2,6},{4,0},{6,2},{1,5},{3,7},{5,1},{7,3},{8,12},{10,14},{12... | collective-permute-start | bytes 1622024 | tf_op jit(solution)/shard_map/ppermute | solution.py:38
  181.6 27.1 %collective-permute-start.9 = (bf16[176,1536]{1,0:T(8,128)(2,1)S(1)}, bf16[176,1536]{1,0:T(8,128)(2,1)S(1)}, u32[]{:S(2)}, u32[]{:S(2)}) collective-permute-start(bf16[176,1536]{1,0:T(8,128)(2,1)S(1)} %add_convert_fusion.1), channel_id=1, source_target_pairs={{0,2},{2,0},{4,6},{6,4},{1,3},{3,1},{5,7},{7,5},{8,10},{10,8},{12,... | collective-permute-start | bytes 1622024 | tf_op jit(solution)/shard_map/ppermute | solution.py:38
  220.7 1.7 copy-start.1

commit v2 on v1

v2 whole, which is shorter than its diff:
```python
import functools
import math

import jax
import jax.numpy as jnp
from jax import lax
from jax.experimental import pallas as pl
from jax.experimental.pallas import tpu as pltpu
from jax.sharding import PartitionSpec as P


VMEM = pl.BlockSpec(memory_space=pltpu.VMEM)
ANY = pl.BlockSpec(memory_space=pl.ANY)
HBM = pl.BlockSpec(memory_space=pltpu.HBM)
GRANT = 12 * 1024 * 1024
BATCHES = (((0, 0), (2, 0)), ((2, 1), (1, 0)), ((3, 0), (3, 1)))
MIX = (2, 1, 0, 3)
SPLIT = {2: 2, 3: 2}
HOLD = ((2, 0),)


def hold(arrays):
    return [pltpu.with_memory_space_constraint(array, pltpu.VMEM) for array in arrays]


def call(body, outs, scratch=(), flops=0, moved=0, grant=GRANT, **specs):
    return pl.pallas_call(
        body,
        out_specs=[VMEM] * len(outs),
        out_shape=outs,
        scratch_shapes=scratch,
        compiler_params=pltpu.CompilerParams(vmem_limit_bytes=grant),
        cost_estimate=pl.CostEstimate(flops=flops, bytes_accessed=moved, transcendentals=0),
        **specs,
    )


def tile_of(size):
    for tile in (512, 384, 256, 128):
        if size % tile == 0:
            return tile
    return size


def send_kernel(layout, experts_ref, mixing_ref, tokens_ref, table_ref, *out_refs):
    capacity, pieces = layout
    rows = tokens_ref.shape[0]
    me = lax.axis_index("expert")
    first = experts_ref[0:1, :]
    second = experts_ref[1:2, :]
    earlier = lax.broadcasted_iota(jnp.int32, (rows, rows), 0) < lax.broadcasted_iota(
        jnp.int32, (rows, rows), 1
    )
    earlier = earlier.astype(jnp.float32).astype(jnp.bfloat16)
    offsets = sorted({start // capacity for start, _ in pieces})
    first_slot = jnp.zeros((1, rows), jnp.int32)
    second_slot = jnp.zeros((1, rows), jnp.int32)
    for offset in offsets:
        expert = me ^ offset
        named = (first == expert) | (second == expert)
        marks = jnp.broadcast_to(named.astype(jnp.float32), (16, rows)).astype(jnp.bfloat16)
        rank = jnp.dot(marks, earlier, preferred_element_type=jnp.float32)[0:1, :]
        slot = rank.astype(jnp.int32) + offset * capacity
        first_slot = jnp.where(first == expert, slot, first_slot)
        second_slot = jnp.where(second == expert, slot, second_slot)
        slot = jnp.where(named, slot, -1)
        for (start, size), out_ref in zip(pieces, out_refs):
            if start // capacity == offset:
                places = lax.broadcasted_iota(jnp.int32, (size, rows), 0) + start
                placing = (slot == places).astype(jnp.float32).astype(jnp.bfloat16)
                out_ref[...] = jnp.dot(
                    placing, tokens_ref[...], preferred_element_type=jnp.float32
                ).astype(out_ref.dtype)
    lines = [
        first_slot.astype(jnp.float32),
        second_slot.astype(jnp.float32),
        mixing_ref[0:1, :],
        mixing_ref[1:2, :],
        jnp.zeros((124, rows), jnp.float32),
    ]
    table_ref[...] = jnp.concatenate(lines, axis=0).T


def send_rows(experts, mixing, tokens, capacity, pieces):
    rows, width = tokens.shape
    outs = [jax.ShapeDtypeStruct((rows, 128), jnp.float32)]
    outs += [jax.ShapeDtypeStruct((size, width), tokens.dtype) for _, size in pieces]
    return call(
        functools.partial(send_kernel, (capacity, pieces)),
        outs,
        flops=2 * rows * width * sum(size for _, size in pieces),
        moved=4 * rows * width,
        grant=12 * 1024 * 1024,
    )(experts.T, mixing.T, tokens)


def column_copies(source_ref, held_ref, base, sems):
    size, tile = source_ref.shape[0], held_ref.shape[1]

    def copy(index):
        cols = pl.ds(pl.multiple_of(index * tile, tile), tile)
        rows = pl.ds(pl.multiple_of(base + index * size, math.gcd(base, size)), size)
        return pltpu.make_async_copy(source_ref.at[:, cols], held_ref.at[rows], sems.at[index])

    return copy, source_ref.shape[1] // tile


def load_kernel(up_ref, *refs):
    held_ref, sems = refs[-2:]
    copy, count = column_copies(up_ref, held_ref, 0, sems)
    for index in range(count):
        copy(index).start()
    for index in range(count):
        copy(index).wait()


def load(up_weight, down_weight, after):
    tile = tile_of(math.gcd(up_weight.shape[1], down_weight.shape[1] // 2))
    size = up_weight.size + down_weight.size
    source = pltpu.with_memory_space_constraint(up_weight, pltpu.HBM)
    return call(
        load_kernel,
        [pltpu.VMEM((size // tile, tile), up_weight.dtype)],
        [pltpu.SemaphoreType.DMA((up_weight.shape[1] // tile,))],
        moved=2 * up_weight.size,
        flops=8 * 10**9,
        in_specs=[HBM] + [ANY] * len(after),
    )(source, *after)[0]


def expert_kernel(sizes, first, *refs):
    count = len(sizes)
    own_refs, other_refs, refs = refs[:count], refs[count : 2 * count], refs[2 * count :]
    weight_ref, refs = refs[0], refs[1:]
    if first:
        down_ref, refs = refs[0], refs[1:]
    send_refs, keep_refs = refs[:count], refs[count : 2 * count]
    rows_ref, hidden_ref = refs[-3:-1] if first else refs[-2:]
    if first:
        weight_ref = refs[2 * count]
    width = own_refs[0].shape[1]
    units = hidden_ref.shape[1]
    tile = weight_ref.shape[1]
    base = weight_ref.shape[0] - 2 * width // tile * units
    if first:
        copy, copies = column_copies(down_ref, weight_ref, base, refs[-1])
        for index in range(copies):
            copy(index).start()
    me = lax.axis_index("etp")
    mine = pl.ds(pl.multiple_of(me * width, width), width)
    theirs = pl.ds(pl.multiple_of((1 - me) * width, width), width)
    row = 0
    for own_ref, other_ref, size in zip(own_refs, other_refs, sizes):
        rows_ref[row : row + size, mine] = own_ref[...]
        rows_ref[row : row + size, theirs] = other_ref[...]
        row += size

    def up_step(index, carry):
        cols = pl.ds(pl.multiple_of(index * tile, tile), tile)
        source = pl.ds(pl.multiple_of(index * 2 * width, 2 * width), 2 * width)
        up_proj = jnp.dot(rows_ref[...], weight_ref[source], preferred_element_type=jnp.float32)
        hidden_ref[:, cols] = (up_proj / (1.0 + jnp.exp(-up_proj))).astype(hidden_ref.dtype)
        return carry

    lax.fori_loop(0, units // tile, up_step, 0)

    def down_piece(index, half, out_refs):
        cols = pl.ds(pl.multiple_of(index * tile, tile), tile)
        position = half * (width // tile) + index
        if first:
            copy(position).wait()
        start = base + position * units
        source = pl.ds(pl.multiple_of(start, math.gcd(base, units)), units)
        sums = jnp.dot(hidden_ref[...], weight_ref[source], preferred_element_type=jnp.float32)
        row = 0
        for out_ref, size in zip(out_refs, sizes):
            out_ref[:, cols] = sums[row : row + size].astype(out_ref.dtype)
            row += size

    def send_step(index, carry):
        down_piece(index, 1 - me, send_refs)
        return carry

    def keep_step(index, carry):
        down_piece(index, me, keep_refs)
        return carry

    lax.fori_loop(0, width // tile, send_step, 0)
    lax.fori_loop(0, width // tile, keep_step, 0)


def expert(own, other, weight, units, down_weight=None):
    sizes = [piece.shape[0] for piece in own]
    rows, width = sum(sizes), own[0].shape[1]
    count = len(sizes)
    first = down_weight is not None
    outs = [jax.ShapeDtypeStruct((size, width), own[0].dtype) for size in sizes * 2]
    scratch = [pltpu.VMEM((rows, 2 * width), own[0].dtype), pltpu.VMEM((rows, units), own[0].dtype)]
    operands = [*own, *other, *hold([weight])]
    specs = {}
    if first:
        outs.append(pltpu.VMEM(weight.shape, weight.dtype))
        scratch.append(pltpu.SemaphoreType.DMA((2 * width // weight.shape[1],)))
        operands.append(pltpu.with_memory_space_constraint(down_weight, pltpu.HBM))
        specs["in_specs"] = [VMEM] * (2 * count + 1) + [HBM]
        specs["input_output_aliases"] = {2 * count: 2 * count}
    results = call(
        functools.partial(expert_kernel, sizes, first),
        outs,
        scratch,
        flops=8 * rows * width * units,
        moved=8 * width * units,
        **specs,
    )(*operands)
    return results[:count], results[count : 2 * count], results[2 * count :]


def add_kernel(keep_ref, other_ref, *refs):
    sum_ref = refs[-1]
    total = keep_ref[...].astype(jnp.float32) + other_ref[...].astype(jnp.float32)
    sum_ref[...] = total.astype(sum_ref.dtype)


def add(keep, other, held):
    size = keep.size
    return call(
        add_kernel, [jax.ShapeDtypeStruct(other.shape, other.dtype)], flops=size, moved=8 * size
    )(keep, other, *hold(held))[0]


def mix_kernel(starts, first, table_ref, *refs):
    out_ref = refs[-1]
    row_refs = refs[: len(starts)]
    rows = table_ref.shape[0]
    total = None if first else refs[len(starts)][...]
    for start, row_ref in zip(starts, row_refs):
        places = lax.broadcasted_iota(jnp.int32, (rows, row_ref.shape[0]), 1) + start
        for k in range(2):
            taking = (table_ref[:, k : k + 1].astype(jnp.int32) == places).astype(jnp.float32).astype(jnp.bfloat16)
            taken = jnp.dot(taking, row_ref[...], preferred_element_type=jnp.float32)
            term = table_ref[:, k + 2 : k + 3] * taken
            total = term if total is None else total + term
    out_ref[...] = total.astype(out_ref.dtype)


def mix(table, parts, starts, total, dtype):
    rows, width = table.shape[0], parts[0].shape[1]
    count = sum(part.shape[0] for part in parts)
    return call(
        functools.partial(mix_kernel, starts, total is None),
        [jax.ShapeDtypeStruct((rows, width), dtype)],
        flops=4 * rows * width * count,
        moved=4 * rows * width,
    )(table, *parts, *([] if total is None else [total]))[0]


def cut(capacity, parts):
    if parts == 1 or capacity < 32:
        return [capacity]
    half = (capacity + 31) // 32 * 16
    return [half, capacity - half]


def local(tokens, experts, mixing, up_weight, down_weight):
    tok_rows = experts.shape[0]
    groups = lax.axis_size("expert")
    halves = lax.axis_size("etp")
    capacity = 2 * tok_rows // groups * 11 // 8
    up_slab = up_weight[0]
    down_slab = down_weight[0]
    paired = halves == 2

    def across(rows, offset):
        pairs = [(i, i ^ offset) for i in range(groups)]
        return rows if offset == 0 else lax.ppermute(rows, "expert", pairs)

    def swap(rows):
        return lax.ppermute(rows, "etp", [(0, 1), (1, 0)])

    def exchange(rows):
        gathered = lax.all_gather(rows, "etp", axis=1, tiled=True)
        up_proj = jnp.dot(gathered, up_slab, preferred_element_type=jnp.float32)
        hidden = jax.nn.silu(up_proj).astype(jnp.bfloat16)
        sums = jnp.dot(hidden, down_slab, preferred_element_type=jnp.float32)
        own = lax.psum_scatter(sums, "etp", scatter_dimension=1, tiled=True)
        return own.astype(jnp.bfloat16)

    tuned = paired and groups == len(MIX)
    batches = BATCHES if tuned else [[(k, 0)] for k in range(groups)]
    split = SPLIT if tuned else {}
    spans = {}
    for offset in range(groups):
        start = offset * capacity
        for index, size in enumerate(cut(capacity, split.get(offset, 1))):
            spans[offset, index] = (start, size)
            start += size
    table, *outgoing = send_rows(experts, mixing, tokens, capacity, list(spans.values()))
    outgoing = dict(zip(spans, outgoing))
    if paired:
        held = load(up_slab, down_slab, [outgoing[0, 0]])
    arrived = {(k, i): across(rows, k) for (k, i), rows in outgoing.items()}
    returned = {}
    for number, batch in enumerate(batches):
        own = [arrived[key] for key in batch]
        if paired:
            others = [swap(arrived[k, i]) for k, i in batch]
            more = [] if number else [down_slab]
            send, keep, filled = expert(own, others, held, up_slab.shape[1], *more)
            held = filled[0] if filled else held
            last = number == len(batches) - 1
            own = []
            for (k, i), mine, rows in zip(batch, keep, send):
                other = swap(rows)
                kept = [held] if (k, i) in HOLD and not last else []
                own.append(add(mine, other, kept))
        else:
            own = [exchange(rows) for rows in own]
        for (k, i), rows in zip(batch, own):
            returned[k, i] = across(rows, k)
    total = None
    order = MIX if tuned else range(groups)
    for offset in order:
        keys = [key for key in spans if key[0] == offset]
        total = mix(
            table,
            [returned[key] for key in keys],
            [spans[key][0] for key in keys],
            total,
            tokens.dtype if offset == order[-1] else jnp.float32,
        )
    return total


def solution(mesh):
    placed = (
        P(("dp", "expert"), "etp"),
        P(("dp", "expert"), None),
        P(("dp", "expert"), None),
        P("expert", None, "etp"),
        P("expert", "etp", None),
    )

    return jax.shard_map(
        local, mesh=mesh, in_specs=placed, out_specs=P(("dp", "expert"), "etp"), check_vma=False
    )
```

time: 223 us -> 194 us (0.87)
  the two profiles are of different devices: /device:TPU:0 before, /device:TPU:19 now
where the time goes in v2:
time: 194 us; the launch traced here: 193 us
  waiting for transfers between devices  80.6 us (42%)
  Pallas kernels  69.2 us (36%)
  local copies, waits for them, and re-layouts  21.7 us (11%)
  starting transfers between devices  21.6 us (11%)
    ppermute x10, waiting for transfers between devices, across(): return rows if offset == 0 else lax.ppermute(rows, 'expert', pairs)  74.9 us
    pallas_call x3, Pallas kernels, expert(): call(functools.partial(expert_kernel, sizes, first), outs, scratch, flops...  52.7 us
    unnamed x44, local copies, waits for them, and re-layouts  21.7 us
    ppermute x10, starting transfers between devices, across(): return rows if offset == 0 else lax.ppermute(rows, 'expert', pairs)  11.7 us
    ppermute x12, starting transfers between devices, swap(): return lax.ppermute(rows, 'etp', [(0, 1), (1, 0)])  9.94 us
    pallas_call x1, Pallas kernels, load(): call(load_kernel, [pltpu.VMEM((size // tile, tile), up_weight.dtype)], [p...  8.41 us
    ppermute x12, waiting for transfers between devices, swap(): return lax.ppermute(rows, 'etp', [(0, 1), (1, 0)])  5.72 us
    pallas_call x4, Pallas kernels, mix(): call(functools.partial(mix_kernel, starts, total is None), [jax.ShapeDtyp...  4.26 us
  transfers between devices with their start and end apart: 22, of which 6 were waited for; matrix products, arithmetic and copies ran while one was open for 0% of the time, Pallas kernels for 34%

profile of v2, /device:TPU:19, one launch (start us, length us, event | category | flops | bytes accessed | tf_op | source)
XLA Modules:
  0.0 193.4 jit_solution(749577764981501000)
XLA Ops:
  0.0 1.1 copy-done.8
  1.1 0.7 copy-done.9
  1.8 0.7 copy-done.10
  2.5 1.5 shard_map.55
  4.0 0.1 collective-permute-start.4
  4.1 2.3 %collective-permute-start.12 = (bf16[80,1536]{1,0:T(8,128)(2,1)S(1)}, bf16[80,1536]{1,0:T(8,128)(2,1)S(1)}, u32[]{:S(2)}, u32[]{:S(2)}) collective-permute-start(bf16[80,1536]{1,0:T(8,128)(2,1)S(1)} %get-tuple-element.37), channel_id=1, source_target_pairs={{0,4},{2,6},{4,0},{6,2},{1,5},{3,7},{5,1},{7,3},{8,12},{10,14},{12... | collective-permute-start | bytes 737288 | tf_op jit(solution)/shard_map/ppermute | solution.py:275
  6.4 1.2 collective-permute-start.5
  7.7 1.3 collective-permute-start.13
  9.0 17.8 %collective-permute-done.12.refs_0_ = bf16[80,1536]{1,0:T(8,128)(2,1)S(1)} collective-permute-done((bf16[80,1536]{1,0:T(8,128)(2,1)S(1)}, bf16[80,1536]{1,0:T(8,128)(2,1)S(1)}, u32[]{:S(2)}, u32[]{:S(2)}) %collective-permute-start.12) | collective-permute-done | bytes 245792 | tf_op jit(solution)/shard_map/ppermute | solution.py:275
  26.7 3.9 %collective-permute-start.1 = (bf16[80,1536]{1,0:T(8,128)(2,1)S(1)}, bf16[80,1536]{1,0:T(8,128)(2,1)}, u32[]{:S(2)}, u32[]{:S(2)}) collective-permute-start(bf16[80,1536]{1,0:T(8,128)(2,1)S(1)} %get-tuple-element.27), channel_id=1, source_target_pairs={{0,6},{2,4},{4,2},{6,0},{1,7},{3,5},{5,3},{7,1},{8,14},{10,12},{12... | collective-permute-start | bytes 737288 | tf_op jit(solution)/shard_map/ppermute | solution.py:275
  30.6 1.2 collective-permute-start.6
  31.8 8.4 %shard_map.56.refs_4_ = bf16[49152,512]{1,0:T(8,128)(2,1)S(1)} custom-call(bf16[3072,4096]{1,0:T(8,128)(2,1)} %bitcast.7, bf16[176,1536]{1,0:T(8,128)(2,1)} %copy-done.2), custom_call_target="tpu_custom_call" | custom-call | flops 8000000000 | bytes 25165824 | tf_op jit(solution)/shard_map/pallas_call | solution.py:121
  40.3 13.8 %collective-permute-done.1.refs_1_ = bf16[80,1536]{1,0:T(8,128)(2,1)} collective-permute-done((bf16[80,1536]{1,0:T(8,128)(2,1)S(1)}, bf16[80,1536]{1,0:T(8,128)(2,1)}, u32[]{:S(2)}, u32[]{:S(2)}) %collective-permute-start.1) | collective-permute-done | bytes 245792 | tf_op jit(solution)/shard_map/ppermute | solution.py:275
  54.1 1.2 collective-permute-start.14
  55.3 0.2 collective-permute-start.3
  55.5 0.0 collective-permute-done.5.refs_2_
  55.6 1.2 collective-permute-start.2
  56.8 0.2 collective-permute-start.15
  57.0 0.0 collective-permute-done.6.refs_3_
  57.0 0.7 copy-done.15
  57.7 19.3 %shard_map.57 = (bf16[176,1536]{1,0:T(8,128)(2,1)}, bf16[96,1536]{1,0:T(8,128)(2,1)}, bf16[176,1536]{1,0:T(8,128)(2,1)}, bf16[96,1536]{1,0:T(8,128)(2,1)}, bf16[49152,512]{1,0:T(8,128)(2,1)S(1)}) custom-call(bf16[176,1536]{1,0:T(8,128)(2,1)} %copy-done.2, bf16[96,1536]{1,0:T(8,128)(2,1)} %copy-done.14, ...), custom_call_target="tpu_custom_call", output_to_operand_aliasing={{4}: (4, {})} | custom-call | flops 13690208256 | bytes 50331648 | tf_op jit(solution)/shard_map/pallas_call | solution.py:207
  77.0 1.3 collective-permute-start.18
  78.4 0.0 collective-permute-done.14.refs_2_
  78.4 0.2 collective-permute-start.11
  78.6 5.7 %collective-permute-done.15.refs_3_ = bf16[176,1536]{1,0:T(8,128)(2,1)S(1)} collective-permute-done((bf16[176,1536]{1,0:T(8,128)(2,1)S(1)}, bf16[176,1536]{1,0:T(8,128)(2,1)S(1)}, u32[]{:S(2)}, u32[]{:S(2)}) %collective-permute-start.15) | collective-permute-done | bytes 540704 | tf_op jit(solution)/shard_map/ppermute | solution.py:278
  84.3 1.9 copy-done.13
  86.2 19.4 %shard_map.62 = (bf16[80,1536]{1,0:T(8,128)(2,1)}, bf16[176,1536]{1,0:T(8,128)(2,1)}, bf16[80,1536]{1,0:T(8,128)(2,1)}, bf16[176,1536]{1,0:T(8,128)(2,1)}) custom-call(bf16[80,1536]{1,0:T(8,128)(2,1)} %copy-done.19, bf16[176,1536]{1,0:T(8,128)(2,1)} %copy-done.12, bf16[80,1536]{1,0:T(8,128)(2,1)} %copy-done.20, bf16[176,1536]{1,0:T(8,128)(2,1)} %copy-done.13, ...), custom_call_target="tpu_custom_call" | custom-call | flops 12884901888 | bytes 50331648 | tf_op jit(solution)/shard_map/pallas_call | solution.py:207
  105.6 1.2 collective-permute-start.16
  106.9 0.0 collective-permute-done.3.refs_3_
  106.9 0.0 collective-permute-done.2.refs_2_
  106.9 0.0 copy-done
  106.9 0.0 copy-start.18
  106.9 0.7 copy-done.18
  107.6 14.0 %shard_map.58 = (bf16[96,1536]{1,0:T(8,128)(2,1)}, bf16[80,1536]{1,0:T(8,128)(2,1)}, bf16[96,1536]{1,0:T(8,128)(2,1)}, bf16[80,1536]{1,0:T(8,128)(2,1)}) custom-call(bf16[96,1536]{1,0:T(8,128)(2,1)} %copy-done.16, bf16[80,1536]{1,0:T(8,128)(2,1)} %collective-permute-done.1.refs_1_, bf16[96,1536]{1,0:T(8,128)(2,1)} %copy-done.18, ...), custom_call_target="tpu_custom_call" | custom-call | flops 8858370048 | bytes 50331648 | tf_op jit(solution)/shard_map/pallas_call | solution.py:207
  121.6 0.2 collective-permute-start.20
  121.8 1.2 collective-permute-start.7
  123.0 0.0 collective-permute-done.16.other_ref
  123.0 0.1 shard_map.63
  123.2 0.1 collective-permute-start.17
  123.2 0.0 collective-permute-done.18.other_ref
  123.2 0.0 copy-start.17
  123.3 0.3 collective-permute-start.9
  123.5 0.4 copy-done.17
  124.0 15.4 %copy-done.1 = bf16[49152,512]{1,0:T(8,128)(2,1)S(1)} copy-done((bf16[49152,512]{1,0:T(8,128)(2,1)S(1)}, bf16[49152,512]{1,0:T(8,128)(2,1)}, u32[]{:S(2)}) %copy-start.1) | copy-done | bytes 50331672
  139.4 1.9 %shard_map.64 = bf16[96,1536]{1,0:T(8,128)(2,1)} custom-call(bf16[96,1536]{1,0:T(8,128)(2,1)} %get-tuple-element.41.keep_ref, bf16[96,1536]{1,0:T(8,128)(2,1)} %copy-done.17, bf16[49152,512]{1,0:T(8,128)(2,1)S(1)} %copy-done.1), custom_call_target="tpu_custom_call" | custom-call | flops 147456 | bytes 1179648 | tf_op jit(solution)/shard_map/pallas_call | solution.py:226
  141.3 0.0 collective-permute-done.20.other_ref
  141.3 0.3 collective-permute-start.19
  141.7 0.1 shard_map.65
  141.7 0.0 collective-permute-done.7.other_ref
  141.7 2.1 %collective-permute-start.21 = (bf16[80,1536]{1,0:T(8,128)(2,1)S(1)}, bf16[80,1536]{1,0:T(8,128)(2,1)S(1)}, u32[]{:S(2)}, u32[]{:S(2)}) collective-permute-start(bf16[80,1536]{1,0:T(8,128)(2,1)S(1)} %shard_map.65), channel_id=1, source_target_pairs={{0,4},{2,6},{4,0},{6,2},{1,5},{3,7},{5,1},{7,3},{8,12},{10,14},{12... | collective-permute-start | bytes 737288 | tf_op jit(solution)/shard_map/ppermute | solution.py:275
  143.8 0.1 shard_map.59
  143.9 0.0 collective-permute-done.9.other_ref
  143.9 0.4 collective-permute-start.8
  144.3 0.1 shard_map.60
  144.4 1.2 collective-permute-start.10
  145.6 0.1 shard_map.61.refs_0_
  145.7 25.3 %collective-permute-done.19.refs_0_ = bf16[96,1536]{1,0:T(8,128)(2,1)S(1)} collective-permute-done((bf16[96,1536]{1,0:T(8,128)(2,1)}, bf16[96,1536]{1,0:T(8,128)(2,1)S(1)}, u32[]{:S(2)}, u32[]{:S(2)}) %collective-permute-start.19) | collective-permute-done | bytes 294944 | tf_op jit(solution)/shard_map/ppermute | solution.py:275
  171.0 5.2 %collective-permute-done.21.refs_1_ = bf16[80,1536]{1,0:T(8,128)(2,1)S(1)} collective-permute-done((bf16[80,1536]{1,0:T(8,128)(2,1)S(1)}, bf16[80,1536]{1,0:T(8,128)(2,1)S(1)}, u32[]{:S(2)}, u32[]{:S(2)}) %collective-permute-start.21) | collective-permute-done | bytes 245792 | tf_op jit(solution)/shard_map/ppermute | solution.py:275
  176.2 1.0 shard_map.66.refs_1_
  177.2 0.0 collective-permute-done.17.refs_0_
  177.2 0.6 shard_map.67.refs_1_
  177.9 0.6 shard_map.68.refs_2_
  178.5 12.9 %collective-permute-done.10.refs_1_ = bf16[80,1536]{1,0:T(8,128)(2,1)S(1)} collective-permute-done((bf16[80,1536]{1,0:T(8,128)(2,1)S(1)}, bf16[80,1536]{1,0:T(8,128)(2,1)S(1)}, u32[]{:S(2)}, u32[]{:S(2)}) %collective-permute-start.10) | collective-permute-done | bytes 245792 | tf_op jit(solution)/shard_map/ppermute | solution.py:275
  191.4 2.0 %shard_map.69 = bf16[256,1536]{1,0:T(8,128)(2,1)} custom-call(f32[256,128]{1,0:T(8,128)S(1)} %get-tuple-element.25.table_ref, bf16[96,1536]{1,0:T(8,128)(2,1)S(1)} %collective-permute-done.8.refs_0_, bf16[80,1536]{1,0:T(8,128)(2,1)S(1)} %collective-permute-done.10.refs_1_, f32[256,1536]{1,0:T(8,128)S(1)} %shard_map.68.refs_2_), custom_call_target="tpu_custom_call" | custom-call | flops 276824064 | bytes 1572864 | tf_op jit(solution)/shard_map/pallas_call | solution.py:249
  (39 shorter events, 0.1 us)
Async XLA Ops:
  0.0 1.1 copy-start.8
  1.1 0.7 copy-start.9
  1.8 0.7 copy-start.10
  4.0 27.9 %copy-start.2 = (bf16[176,1536]{1,0:T(8,128)(2,1)}, bf16[176,1536]{1,0:T(8,128)(2,1)S(1)}, u32[]{:S(2)}) copy-start(bf16[176,1536]{1,0:T(8,128)(2,1)S(1)} %get-tuple-element.28.refs_0_) | copy-start | bytes 1622020
  4.0 26.6 %collective-permute-start.4 = (bf16[96,1536]{1,0:T(8,128)(2,1)S(1)}, bf16[96,1536]{1,0:T(8,128)(2,1)S(1)}, u32[]{:S(2)}, u32[]{:S(2)}) collective-permute-start(bf16[96,1536]{1,0:T(8,128)(2,1)S(1)} %get-tuple-element.29), channel_id=1, source_target_pairs={{0,4},{2,6},{4,0},{6,2},{1,5},{3,7},{5,1},{7,3},{8,12},{10,14},{12... | collective-permute-start | bytes 884744 | tf_op jit(solution)/shard_map/ppermute | solution.py:275
  4.1 22.6 %collective-permute-start.12 = (bf16[80,1536]{1,0:T(8,128)(2,1)S(1)}, bf16[80,1536]{1,0:T(8,128)(2,1)S(1)}, u32[]{:S(2)}, u32[]{:S(2)}) collective-permute-start(bf16[80,1536]{1,0:T(8,128)(2,1)S(1)} %get-tuple-element.37), channel_id=1, source_target_pairs={{0,4},{2,6},{4,0},{6,2},{1,5},{3,7},{5,1},{7,3},{8,12},{10,14},{12... | collective-permute-start | bytes 737288 | tf_op jit(solution)/shard_map/ppermute | solution.py:275
  6.4 49.1 %collective-permute-start.5 = (bf16[176,1536]{1,0:T(8,128)(2,1)S(1)}, bf16[176,1536]{1,0:T(8,128)(2,1)S(1)}, u32[]{:S(2)}, u32[]{:S(2)}) collective-permute-start(bf16[176,1536]{1,0:T(8,128)(2,1)S(1)} %get-tuple-element.28.refs_0_), channel_id=1, source_target_pairs={{0,1},{1,0},{2,3},{3,2},{4,5},{5,4},{6,7},{7,6},{8,9},{9,8},{10,11... | collective-permute-start | bytes 1622024 | tf_op jit(solution)/shard_map/ppermute | solution.py:278
  7.7 49.1 %collective-permute-start.13 = (bf16[176,1536]{1,0:T(8,128)(2,1)S(1)}, bf16[176,1536]{1,0:T(8,128)(2,1)S(1)}, u32[]{:S(2)}, u32[]{:S(2)}) collective-permute-start(bf16[176,1536]{1,0:T(8,128)(2,1)S(1)} %get-tuple-element.38), channel_id=1, source_target_pairs={{0,2},{2,0},{4,6},{6,4},{1,3},{3,1},{5,7},{7,5},{8,10},{10,8},{12,... | collective-permute-start | bytes 1622024 | tf_op jit(solution)/shard_map/ppermute | solution.py:275
  9.0 46.4 %collective-permute-start = (bf16[96,1536]{1,0:T(8,128)(2,1)S(1)}, bf16[96,1536]{1,0:T(8,128)(2,1)S(1)}, u32[]{:S(2)}, u32[]{:S(2)}) collective-permute-start(bf16[96,1536]{1,0:T(8,128)(2,1)S(1)} %get-tuple-element.26), channel_id=1, source_target_pairs={{0,6},{2,4},{4,2},{6,0},{1,7},{3,5},{5,3},{7,1},{8,14},{10,12},{12... | collective-permute-start | bytes 884744 | tf_op jit(solution)/shard_map/ppermute | solution.py:275
  26.7 27.3 %copy-start.19 = (bf16[80,1536]{1,0:T(8,128)(2,1)}, bf16[80,1536]{1,0:T(8,128)(2,1)S(1)}, u32[]{:S(2)}) copy-start(bf16[80,1536]{1,0:T(8,128)(2,1)S(1)} %collective-permute-done.12.refs_0_) | copy-start | bytes 737284
  26.7 27.3 %collective-permute-start.1 = (bf16[80,1536]{1,0:T(8,128)(2,1)S(1)}, bf16[80,1536]{1,0:T(8,128)(2,1)}, u32[]{:S(2)}, u32[]{:S(2)}) collective-permute-start(bf16[80,1536]{1,0:T(8,128)(2,1)S(1)} %get-tuple-element.27), channel_id=1, source_target_pairs={{0,6},{2,4},{4,2},{6,0},{1,7},{3,5},{5,3},{7,1},{8,14},{10,12},{12... | collective-permute-start | bytes 737288 | tf_op jit(solution)/shard_map/ppermute | solution.py:275
  30.6 9.7 %copy-start.14 = (bf16[96,1536]{1,0:T(8,128)(2,1)}, bf16[96,1536]{1,0:T(8,128)(2,1)S(1)}, u32[]{:S(2)}) copy-start(bf16[96,1536]{1,0:T(8,128)(2,1)S(1)} %collective-permute-done.4.refs_1_) | copy-start | bytes 884740
  30.6 26.4 %collective-permute-start.6 = (bf16[96,1536]{1,0:T(8,128)(2,1)S(1)}, bf16[96,1536]{1,0:T(8,128)(2,1)S(1)}, u32[]{:S(2)}, u32[]{:S(2)}) collective-permute-start(bf16[96,1536]{1,0:T(8,128)(2,1)S(1)} %collective-permute-done.4.refs_1_), channel_id=1, source_target_pairs={{0,1},{1,0},{2,3},{3,2},{4,5},{5,4},{6,7},{7,6},{8,9},{9,8},{10,11... | collective-permute-start | bytes 884744 | tf_op jit(solution)/shard_map/ppermute | solution.py:278
  54.1 24.3 %collective-permute-start.14 = (bf16[80,1536]{1,0:T(8,128)(2,1)S(1)}, bf16[80,1536]{1,0:T(8,128)(2,1)S(1)}, u32[]{:S(2)}, u32[]{:S(2)}) collective-permute-start(bf16[80,1536]{1,0:T(8,128)(2,1)S(1)} %collective-permute-done.12.refs_0_), channel_id=1, source_target_pairs={{0,1},{1,0},{2,3},{3,2},{4,5},{5,4},{6,7},{7,6},{8,9},{9,8},{10,11... | collective-permute-start | bytes 737288 | tf_op jit(solution)/shard_map/ppermute | solution.py:278
  55.3 51.5 %copy-start.16 = (bf16[96,1536]{1,0:T(8,128)(2,1)}, bf16[96,1536]{1,0:T(8,128)(2,1)S(1)}, u32[]{:S(2)}) copy-start(bf16[96,1536]{1,0:T(8,128)(2,1)S(1)} %collective-permute-done.refs_0_) | copy-start | bytes 884740
  55.3 51.5 %collective-permute-start.3 = (bf16[80,1536]{1,0:T(8,128)(2,1)}, bf16[80,1536]{1,0:T(8,128)(2,1)}, u32[]{:S(2)}, u32[]{:S(2)}) collective-permute-start(bf16[80,1536]{1,0:T(8,128)(2,1)} %collective-permute-done.1.refs_1_), channel_id=1, source_target_pairs={{0,1},{1,0},{2,3},{3,2},{4,5},{5,4},{6,7},{7,6},{8,9},{9,8},{10,11... | collective-permute-start | bytes 737288 | tf_op jit(solution)/shard_map/ppermute | solution.py:278
  55.5 1.5 copy-start.11
  55.6 51.3 %collective-permute-start.2 = (bf16[96,1536]{1,0:T(8,128)(2,1)S(1)}, bf16[96,1536]{1,0:T(8,128)(2,1)S(1)}, u32[]{:S(2)}, u32[]{:S(2)}) collective-permute-start(bf16[96,1536]{1,0:T(8,128)(2,1)S(1)} %collective-permute-done.refs_0_), channel_id=1, source_target_pairs={{0,1},{1,0},{2,3},{3,2},{4,5},{5,4},{6,7},{7,6},{8,9},{9,8},{10,11... | collective-permute-start | bytes 884744 | tf_op jit(solution)/shard_map/ppermute | solution.py:278
  56.8 20.2 %copy-start.12 = (bf16[176,1536]{1,0:T(8,128)(2,1)}, bf16[176,1536]{1,0:T(8,128)(2,1)S(1)}, u32[]{:S(2)}) copy-start(bf16[176,1536]{1,0:T(8,128)(2,1)S(1)} %collective-permute-done.13.refs_1_) | copy-start | bytes 1622020
  56.8 27.5 %collective-permute-start.15 = (bf16[176,1536]{1,0:T(8,128)(2,1)S(1)}, bf16[176,1536]{1,0:T(8,128)(2,1)S(1)}, u32[]{:S(2)}, u32[]{:S(2)}) collective-permute-start(bf16[176,1536]{1,0:T(8,128)(2,1)S(1)} %collective-permute-done.13.refs_1_), channel_id=1, source_target_pairs={{0,1},{1,0},{2,3},{3,2},{4,5},{5,4},{6,7},{7,6},{8,9},{9,8},{10,11... | collective-permute-start | bytes 1622024 | tf_op jit(solution)/shard_map/ppermute | solution.py:278
  57.0 0.7 copy-start.15
  77.0 29.8 %copy-start = (bf16[49152,512]{1,0:T(8,128)(2,1)}, bf16[49152,512]{1,0:T(8,128)(2,1)S(1)}, u32[]{:S(2)}) copy-start(bf16[49152,512]{1,0:T(8,128)(2,1)S(1)} %get-tuple-element.30.refs_4_.refs_0_) | copy-start | bytes 150994944
  77.0 46.2 %collective-permute-start.18 = (bf16[96,1536]{1,0:T(8,128)(2,1)}, bf16[96,1536]{1,0:T(8,128)(2,1)S(1)}, u32[]{:S(2)}, u32[]{:S(2)}) collective-permute-start(bf16[96,1536]{1,0:T(8,128)(2,1)} %get-tuple-element.42), channel_id=1, source_target_pairs={{0,1},{1,0},{2,3},{3,2},{4,5},{5,4},{6,7},{7,6},{8,9},{9,8},{10,11... | collective-permute-start | bytes 884744 | tf_op jit(solution)/shard_map/ppermute | solution.py:278
  78.4 5.9 %copy-start.20 = (bf16[80,1536]{1,0:T(8,128)(2,1)}, bf16[80,1536]{1,0:T(8,128)(2,1)S(1)}, u32[]{:S(2)}) copy-start(bf16[80,1536]{1,0:T(8,128)(2,1)S(1)} %collective-permute-done.14.refs_2_) | copy-start | bytes 737284
  78.4 66.0 %collective-permute-start.11 = (bf16[176,1536]{1,0:T(8,128)(2,1)}, bf16[176,1536]{1,0:T(8,128)(2,1)S(1)}, u32[]{:S(2)}, u32[]{:S(2)}) collective-permute-start(bf16[176,1536]{1,0:T(8,128)(2,1)} %get-tuple-element.36), channel_id=1, source_target_pairs={{0,1},{1,0},{2,3},{3,2},{4,5},{5,4},{6,7},{7,6},{8,9},{9,8},{10,11... | collective-permute-start | bytes 1622024 | tf_op jit(solution)/shard_map/ppermute | solution.py:278
  84.3 1.9 copy-start.13
  105.6 15.9 %copy-start.21 = (bf16[80,1536]{1,0:T(8,128)(2,1)S(1)}, bf16[80,1536]{1,0:T(8,128)(2,1)}, u32[]{:S(2)}) copy-start(bf16[80,1536]{1,0:T(8,128)(2,1)} %get-tuple-element.44) | copy-start | bytes 737284
  105.6 17.4 %copy-start.4 = (bf16[176,1536]{1,0:T(8,128)(2,1)S(1)}, bf16[176,1536]{1,0:T(8,128)(2,1)}, u32[]{:S(2)}) copy-start(bf16[176,1536]{1,0:T(8,128)(2,1)} %get-tuple-element.39.keep_ref) | copy-start | bytes 1622020
  105.6 17.4 %collective-permute-start.16 = (bf16[176,1536]{1,0:T(8,128)(2,1)}, bf16[176,1536]{1,0:T(8,128)(2,1)S(1)}, u32[]{:S(2)}, u32[]{:S(2)}) collective-permute-start(bf16[176,1536]{1,0:T(8,128)(2,1)} %get-tuple-element.40), channel_id=1, source_target_pairs={{0,1},{1,0},{2,3},{3,2},{4,5},{5,4},{6,7},{7,6},{8,9},{9,8},{10,11... | collective-permute-start | bytes 1622024 | tf_op jit(solution)/shard_map/ppermute | solution.py:278
  106.9 0.7 copy-start.18
  121.6 19.8 %collective-permute-start.20 = (bf16[80,1536]{1,0:T(8,128)(2,1)S(1)}, bf16[80,1536]{1,0:T(8,128)(2,1)S(1)}, u32[]{:S(2)}, u32[]{:S(2)}) collective-permute-start(bf16[80,1536]{1,0:T(8,128)(2,1)S(1)} %copy-done.21), channel_id=1, source_target_pairs={{0,1},{1,0},{2,3},{3,2},{4,5},{5,4},{6,7},{7,6},{8,9},{9,8},{10,11... | collective-permute-start | bytes 737288 | tf_op jit(solution)/shard_map/ppermute | solution.py:278
  121.8 20.0 %collective-permute-start.7 = (bf16[96,1536]{1,0:T(8,128)(2,1)}, bf16[96,1536]{1,0:T(8,128)(2,1)S(1)}, u32[]{:S(2)}, u32[]{:S(2)}) collective-permute-start(bf16[96,1536]{1,0:T(8,128)(2,1)} %get-tuple-element.32), channel_id=1, source_target_pairs={{0,1},{1,0},{2,3},{3,2},{4,5},{5,4},{6,7},{7,6},{8,9},{9,8},{10,11... | collective-permute-start | bytes 884744 | tf_op jit(solution)/shard_map/ppermute | solution.py:278
  123.2 54.1 %collective-permute-start.17 = (bf16[176,1536]{1,0:T(8,128)(2,1)S(1)}, bf16[176,1536]{1,0:T(8,128)(2,1)S(1)}, u32[]{:S(2)}, u32[]{:S(2)}) collective-permute-start(bf16[176,1536]{1,0:T(8,128)(2,1)S(1)} %shard_map.63), channel_id=1, source_target_pairs={{0,2},{2,0},{4,6},{6,4},{1,3},{3,1},{5,7},{7,5},{8,10},{10,8},{12,... | collective-permute-start | bytes 1622024 | tf_op jit(solution)/shard_map/ppermute | solution.py:275
  123.2 0.7 copy-start.17
  123.3 20.7 %collective-permute-start.9 = (bf16[80,1536]{1,0:T(8,128)(2,1)}, bf16[80,1536]{1,0:T(8,128)(2,1)S(1)}, u32[]{:S(2)}, u32[]{:S(2)}) collective-permute-start(bf16[80,1536]{1,0:T(8,128)(2,1)} %get-tuple-element.34), channel_id=1, source_target_pairs={{0,1},{1,0},{2,3},{3,2},{4,5},{5,4},{6,7},{7,6},{8,9},{9,8},{10,11... | collective-permute-start | bytes 737288 | tf_op jit(solution)/shard_map/ppermute | solution.py:278
  124.0 15.4 %copy-start.1 = (bf16[49152,512]{1,0:T(8,128)(2,1)S(1)}, bf16[49152,512]{1,0:T(8,128)(2,1)}, u32[]{:S(2)}) copy-start(bf16[49152,512]{1,0:T(8,128)(2,1)} %copy-done) | copy-start | bytes 150994944
  139.4 2.3 %copy-start.7 = (bf16[80,1536]{1,0:T(8,128)(2,1)S(1)}, bf16[80,1536]{1,0:T(8,128)(2,1)}, u32[]{:S(2)}) copy-start(bf16[80,1536]{1,0:T(8,128)(2,1)} %get-tuple-element.43.keep_ref) | copy-start | bytes 737284
  139.4 4.5 %copy-start.5 = (bf16[96,1536]{1,0:T(8,128)(2,1)S(1)}, bf16[96,1536]{1,0:T(8,128)(2,1)}, u32[]{:S(2)}) copy-start(bf16[96,1536]{1,0:T(8,128)(2,1)} %get-tuple-element.31.keep_ref) | copy-start | bytes 884740
  139.4 4.9 %copy-start.6 = (bf16[80,1536]{1,0:T(8,128)(2,1)S(1)}, bf16[80,1536]{1,0:T(8,128)(2,1)}, u32[]{:S(2)}) copy-start(bf16[80,1536]{1,0:T(8,128)(2,1)} %get-tuple-element.33.keep_ref) | copy-start | bytes 737284
  139.4 6.2 %copy-start.3 = (bf16[176,1536]{1,0:T(8,128)(2,1)S(1)}, bf16[176,1536]{1,0:T(8,128)(2,1)}, u32[]{:S(2)}) copy-start(bf16[176,1536]{1,0:T(8,128)(2,1)} %get-tuple-element.35.keep_ref) | copy-start | bytes 1622020
  141.3 29.7 %collective-permute-start.19 = (bf16[96,1536]{1,0:T(8,128)(2,1)}, bf16[96,1536]{1,0:T(8,128)(2,1)S(1)}, u32[]{:S(2)}, u32[]{:S(2)}) collective-permute-start(bf16[96,1536]{1,0:T(8,128)(2,1)} %shard_map.64), channel_id=1, source_target_pairs={{0,4},{2,6},{4,0},{6,2},{1,5},{3,7},{5,1},{7,3},{8,12},{10,14},{12... | collective-permute-start | bytes 884744 | tf_op jit(solution)/shard_map/ppermute | solution.py:275
  141.7 34.5 %collective-permute-start.21 = (bf16[80,1536]{1,0:T(8,128)(2,1)S(1)}, bf16[80,1536]{1,0:T(8,128)(2,1)S(1)}, u32[]{:S(2)}, u32[]{:S(2)}) collective-permute-start(bf16[80,1536]{1,0:T(8,128)(2,1)S(1)} %shard_map.65), channel_id=1, source_target_pairs={{0,4},{2,6},{4,0},{6,2},{1,5},{3,7},{5,1},{7,3},{8,12},{10,14},{12... | collective-permute-start | bytes 737288 | tf_op jit(solution)/shard_map/ppermute | solution.py:275
  143.9 47.5 %collective-permute-start.8 = (bf16[96,1536]{1,0:T(8,128)(2,1)S(1)}, bf16[96,1536]{1,0:T(8,128)(2,1)S(1)}, u32[]{:S(2)}, u32[]{:S(2)}) collective-permute-start(bf16[96,1536]{1,0:T(8,128)(2,1)S(1)} %shard_map.59), channel_id=1, source_target_pairs={{0,6},{2,4},{4,2},{6,0},{1,7},{3,5},{5,3},{7,1},{8,14},{10,12},{12... | collective-permute-start | bytes 884744 | tf_op jit(solution)/shard_map/ppermute | solution.py:275
  144.4 47.0 %collective-permute-start.10 = (bf16[80,1536]{1,0:T(8,128)(2,1)S(1)}, bf16[80,1536]{1,0:T(8,128)(2,1)S(1)}, u32[]{:S(2)}, u32[]{:S(2)}) collective-permute-start(bf16[80,1536]{1,0:T(8,128)(2,1)S(1)} %shard_map.60), channel_id=1, source_target_pairs={{0,6},{2,4},{4,2},{6,0},{1,7},{3,5},{5,3},{7,1},{8,14},{10,12},{12... | collective-permute-start | bytes 737288 | tf_op jit(solution)/shard_map/ppermute | solution.py:275

commit v3 on v2

--- a/solution.py
+++ b/solution.py
@@ -16,7 +16,7 @@
 BATCHES = (((0, 0), (2, 0)), ((2, 1), (1, 0)), ((3, 0), (3, 1)))
 MIX = (2, 1, 0, 3)
 SPLIT = {2: 2, 3: 2}
-HOLD = ((2, 0),)
+HOLD = ((2, 0), (2, 1))
 
 
 def hold(arrays):
@@ -42,8 +42,18 @@
     return size
 
 
-def send_kernel(layout, experts_ref, mixing_ref, tokens_ref, table_ref, *out_refs):
+def send_kernel(layout, *refs):
     capacity, pieces = layout
+    sources, table_ref, out_refs = refs[:3], refs[3], refs[4:-4]
+    copies = [
+        pltpu.make_async_copy(source, target, refs[-1].at[index])
+        for index, (source, target) in enumerate(zip(sources, refs[-4:-1]))
+    ]
+    for copy in copies:
+        copy.start()
+    for copy in copies:
+        copy.wait()
+    experts_ref, mixing_ref, tokens_ref = refs[-4:-1]
     rows = tokens_ref.shape[0]
     me = lax.axis_index("expert")
     first = experts_ref[0:1, :]
@@ -85,13 +95,17 @@
     rows, width = tokens.shape
     outs = [jax.ShapeDtypeStruct((rows, 128), jnp.float32)]
     outs += [jax.ShapeDtypeStruct((size, width), tokens.dtype) for _, size in pieces]
+    sources = (experts.T, mixing.T, tokens)
+    scratch = [pltpu.VMEM(x.shape, x.dtype) for x in sources]
     return call(
         functools.partial(send_kernel, (capacity, pieces)),
         outs,
+        [*scratch, pltpu.SemaphoreType.DMA((3,))],
         flops=2 * rows * width * sum(size for _, size in pieces),
         moved=4 * rows * width,
         grant=12 * 1024 * 1024,
-    )(experts.T, mixing.T, tokens)
+        in_specs=[HBM] * 3,
+    )(*[pltpu.with_memory_space_constraint(x, pltpu.HBM) for x in sources])
 
 
 def column_copies(source_ref, held_ref, base, sems):

time: 194 us -> 193 us (level)
  the two profiles are of different devices: /device:TPU:19 before, /device:TPU:17 now
where the time goes in v3:
time: 193 us; the launch traced here: 192 us
  waiting for transfers between devices  79.2 us (41%)
  Pallas kernels  72.1 us (37%)
  starting transfers between devices  21 us (11%)
  local copies, waits for them, and re-layouts  19.6 us (10%)
    ppermute x10, waiting for transfers between devices, across(): return rows if offset == 0 else lax.ppermute(rows, 'expert', pairs)  73.3 us
    pallas_call x3, Pallas kernels, expert(): call(functools.partial(expert_kernel, sizes, first), outs, scratch, flops...  52.7 us
    unnamed x36, local copies, waits for them, and re-layouts  19.6 us
    ppermute x10, starting transfers between devices, across(): return rows if offset == 0 else lax.ppermute(rows, 'expert', pairs)  11 us
    ppermute x12, starting transfers between devices, swap(): return lax.ppermute(rows, 'etp', [(0, 1), (1, 0)])  9.94 us
    pallas_call x1, Pallas kernels, load(): call(load_kernel, [pltpu.VMEM((size // tile, tile), up_weight.dtype)], [p...  8.41 us
    ppermute x12, waiting for transfers between devices, swap(): return lax.ppermute(rows, 'etp', [(0, 1), (1, 0)])  5.93 us
    pallas_call x4, Pallas kernels, mix(): call(functools.partial(mix_kernel, starts, total is None), [jax.ShapeDtyp...  4.26 us
  transfers between devices with their start and end apart: 22, of which 6 were waited for; matrix products, arithmetic and copies ran while one was open for 0% of the time, Pallas kernels for 35%

profile of v3, /device:TPU:17, one launch (start us, length us, event | category | flops | bytes accessed | tf_op | source)
XLA Modules:
  0.0 192.2 jit_solution(7307977266314411150)
XLA Ops:
  0.0 2.7 %shard_map.55 = (f32[256,128]{1,0:T(8,128)S(1)}, bf16[176,1536]{1,0:T(8,128)(2,1)S(1)}, bf16[176,1536]{1,0:T(8,128)(2,1)S(1)}, bf16[96,1536]{1,0:T(8,128)(2,1)S(...) custom-call(s32[2,256]{1,0:T(2,128)} %bitcast.6, f32[2,256]{1,0:T(2,128)} %bitcast.7, ...), custom_call_target="tpu_custom_call" | custom-call | flops 553648128 | bytes 1572864 | tf_op jit(solution)/shard_map/pallas_call | solution.py:100
  2.7 0.0 copy-start.2
  2.7 0.1 collective-permute-start.4
  2.8 2.4 %collective-permute-start.12 = (bf16[80,1536]{1,0:T(8,128)(2,1)S(1)}, bf16[80,1536]{1,0:T(8,128)(2,1)}, u32[]{:S(2)}, u32[]{:S(2)}) collective-permute-start(bf16[80,1536]{1,0:T(8,128)(2,1)S(1)} %get-tuple-element.37), channel_id=1, source_target_pairs={{0,4},{2,6},{4,0},{6,2},{1,5},{3,7},{5,1},{7,3},{8,12},{10,14},{12... | collective-permute-start | bytes 737288 | tf_op jit(solution)/shard_map/ppermute | solution.py:289
  5.1 1.2 collective-permute-start.5
  6.4 1.3 collective-permute-start.13
  7.7 0.0 collective-permute-start
  7.7 18.0 %collective-permute-done.12.refs_0_ = bf16[80,1536]{1,0:T(8,128)(2,1)} collective-permute-done((bf16[80,1536]{1,0:T(8,128)(2,1)S(1)}, bf16[80,1536]{1,0:T(8,128)(2,1)}, u32[]{:S(2)}, u32[]{:S(2)}) %collective-permute-start.12) | collective-permute-done | bytes 245792 | tf_op jit(solution)/shard_map/ppermute | solution.py:289
  25.6 3.7 %collective-permute-start.1 = (bf16[80,1536]{1,0:T(8,128)(2,1)S(1)}, bf16[80,1536]{1,0:T(8,128)(2,1)}, u32[]{:S(2)}, u32[]{:S(2)}) collective-permute-start(bf16[80,1536]{1,0:T(8,128)(2,1)S(1)} %get-tuple-element.27), channel_id=1, source_target_pairs={{0,6},{2,4},{4,2},{6,0},{1,7},{3,5},{5,3},{7,1},{8,14},{10,12},{12... | collective-permute-start | bytes 737288 | tf_op jit(solution)/shard_map/ppermute | solution.py:289
  29.3 1.2 collective-permute-start.6
  30.6 8.4 %shard_map.56.refs_4_ = bf16[49152,512]{1,0:T(8,128)(2,1)S(1)} custom-call(bf16[3072,4096]{1,0:T(8,128)(2,1)} %bitcast.5, bf16[176,1536]{1,0:T(8,128)(2,1)} %copy-done.2), custom_call_target="tpu_custom_call" | custom-call | flops 8000000000 | bytes 25165824 | tf_op jit(solution)/shard_map/pallas_call | solution.py:135
  39.0 13.8 %collective-permute-done.1.refs_1_ = bf16[80,1536]{1,0:T(8,128)(2,1)} collective-permute-done((bf16[80,1536]{1,0:T(8,128)(2,1)S(1)}, bf16[80,1536]{1,0:T(8,128)(2,1)}, u32[]{:S(2)}, u32[]{:S(2)}) %collective-permute-start.1) | collective-permute-done | bytes 245792 | tf_op jit(solution)/shard_map/ppermute | solution.py:289
  52.8 1.2 collective-permute-start.14
  54.0 0.0 collective-permute-done.refs_0_
  54.0 0.2 collective-permute-start.3
  54.3 1.2 collective-permute-start.2
  55.5 0.0 collective-permute-done.13.refs_1_
  55.5 0.2 collective-permute-start.15
  55.7 0.7 copy-done.11
  56.4 19.3 %shard_map.57 = (bf16[176,1536]{1,0:T(8,128)(2,1)}, bf16[96,1536]{1,0:T(8,128)(2,1)}, bf16[176,1536]{1,0:T(8,128)(2,1)}, bf16[96,1536]{1,0:T(8,128)(2,1)}, bf16[49152,512]{1,0:T(8,128)(2,1)S(1)}) custom-call(bf16[176,1536]{1,0:T(8,128)(2,1)} %copy-done.2, bf16[96,1536]{1,0:T(8,128)(2,1)} %copy-done.10, ...), custom_call_target="tpu_custom_call", output_to_operand_aliasing={{4}: (4, {})} | custom-call | flops 13690208256 | bytes 50331648 | tf_op jit(solution)/shard_map/pallas_call | solution.py:221
  75.7 1.3 collective-permute-start.18
  77.1 0.0 collective-permute-done.14.refs_2_
  77.1 0.2 collective-permute-start.11
  77.3 5.9 %collective-permute-done.15.refs_3_ = bf16[176,1536]{1,0:T(8,128)(2,1)S(1)} collective-permute-done((bf16[176,1536]{1,0:T(8,128)(2,1)S(1)}, bf16[176,1536]{1,0:T(8,128)(2,1)S(1)}, u32[]{:S(2)}, u32[]{:S(2)}) %collective-permute-start.15) | collective-permute-done | bytes 540704 | tf_op jit(solution)/shard_map/ppermute | solution.py:292
  83.2 1.9 copy-done.9
  85.1 19.4 %shard_map.62 = (bf16[80,1536]{1,0:T(8,128)(2,1)}, bf16[176,1536]{1,0:T(8,128)(2,1)}, bf16[80,1536]{1,0:T(8,128)(2,1)}, bf16[176,1536]{1,0:T(8,128)(2,1)}) custom-call(bf16[80,1536]{1,0:T(8,128)(2,1)} %collective-permute-done.12.refs_0_, bf16[176,1536]{1,0:T(8,128)(2,1)} %copy-done.8, bf16[80,1536]{1,0:T(8,128)(2,1)} %copy-done.15, ...), custom_call_target="tpu_custom_call" | custom-call | flops 12884901888 | bytes 50331648 | tf_op jit(solution)/shard_map/pallas_call | solution.py:221
  104.5 1.2 collective-permute-start.16
  105.8 0.0 collective-permute-done.3.refs_3_
  105.8 0.0 collective-permute-done.2.refs_2_
  105.8 0.0 copy-done
  105.8 0.0 copy-start.14
  105.8 0.7 copy-done.14
  106.5 14.0 %shard_map.58 = (bf16[96,1536]{1,0:T(8,128)(2,1)}, bf16[80,1536]{1,0:T(8,128)(2,1)}, bf16[96,1536]{1,0:T(8,128)(2,1)}, bf16[80,1536]{1,0:T(8,128)(2,1)}) custom-call(bf16[96,1536]{1,0:T(8,128)(2,1)} %copy-done.12, bf16[80,1536]{1,0:T(8,128)(2,1)} %collective-permute-done.1.refs_1_, bf16[96,1536]{1,0:T(8,128)(2,1)} %copy-done.14, ...), custom_call_target="tpu_custom_call" | custom-call | flops 8858370048 | bytes 50331648 | tf_op jit(solution)/shard_map/pallas_call | solution.py:221
  120.5 0.2 collective-permute-start.20
  120.7 1.2 collective-permute-start.7
  122.0 0.1 shard_map.63
  122.1 0.1 collective-permute-start.17
  122.2 0.0 collective-permute-done.18.other_ref
  122.2 0.0 copy-start.13
  122.2 0.3 collective-permute-start.9
  122.5 0.4 copy-done.13
  122.9 15.5 %copy-done.1 = bf16[49152,512]{1,0:T(8,128)(2,1)S(1)} copy-done((bf16[49152,512]{1,0:T(8,128)(2,1)S(1)}, bf16[49152,512]{1,0:T(8,128)(2,1)}, u32[]{:S(2)}) %copy-start.1) | copy-done | bytes 50331672
  138.4 1.8 shard_map.64
  140.2 0.0 collective-permute-done.20.other_ref
  140.2 0.3 collective-permute-start.19
  140.5 0.4 copy-done.16
  140.9 1.9 shard_map.65
  142.8 0.0 collective-permute-done.7.other_ref
  142.8 1.7 collective-permute-start.21
  144.5 0.1 shard_map.59
  144.6 1.0 collective-permute-start.8
  145.6 0.1 shard_map.60
  145.7 0.0 collective-permute-done.11.other_ref
  145.7 0.6 collective-permute-start.10
  146.3 0.1 shard_map.61.refs_0_
  146.4 23.5 %collective-permute-done.19.refs_0_ = bf16[96,1536]{1,0:T(8,128)(2,1)S(1)} collective-permute-done((bf16[96,1536]{1,0:T(8,128)(2,1)}, bf16[96,1536]{1,0:T(8,128)(2,1)S(1)}, u32[]{:S(2)}, u32[]{:S(2)}) %collective-permute-start.19) | collective-permute-done | bytes 294944 | tf_op jit(solution)/shard_map/ppermute | solution.py:289
  169.9 5.3 %collective-permute-done.21.refs_1_ = bf16[80,1536]{1,0:T(8,128)(2,1)S(1)} collective-permute-done((bf16[80,1536]{1,0:T(8,128)(2,1)}, bf16[80,1536]{1,0:T(8,128)(2,1)S(1)}, u32[]{:S(2)}, u32[]{:S(2)}) %collective-permute-start.21) | collective-permute-done | bytes 245792 | tf_op jit(solution)/shard_map/ppermute | solution.py:289
  175.2 1.0 shard_map.66.refs_1_
  176.2 0.0 collective-permute-done.17.refs_0_
  176.2 0.6 shard_map.67.refs_1_
  176.9 0.6 shard_map.68.refs_2_
  177.5 12.8 %collective-permute-done.10.refs_1_ = bf16[80,1536]{1,0:T(8,128)(2,1)S(1)} collective-permute-done((bf16[80,1536]{1,0:T(8,128)(2,1)S(1)}, bf16[80,1536]{1,0:T(8,128)(2,1)S(1)}, u32[]{:S(2)}, u32[]{:S(2)}) %collective-permute-start.10) | collective-permute-done | bytes 245792 | tf_op jit(solution)/shard_map/ppermute | solution.py:289
  190.3 0.0 collective-permute-done.8.refs_0_
  190.3 2.0 %shard_map.69 = bf16[256,1536]{1,0:T(8,128)(2,1)} custom-call(f32[256,128]{1,0:T(8,128)S(1)} %get-tuple-element.25.table_ref, bf16[96,1536]{1,0:T(8,128)(2,1)S(1)} %collective-permute-done.8.refs_0_, bf16[80,1536]{1,0:T(8,128)(2,1)S(1)} %collective-permute-done.10.refs_1_, f32[256,1536]{1,0:T(8,128)S(1)} %shard_map.68.refs_2_), custom_call_target="tpu_custom_call" | custom-call | flops 276824064 | bytes 1572864 | tf_op jit(solution)/shard_map/pallas_call | solution.py:263
  (31 shorter events, 0.1 us)
Async XLA Ops:
  2.7 27.9 %copy-start.2 = (bf16[176,1536]{1,0:T(8,128)(2,1)}, bf16[176,1536]{1,0:T(8,128)(2,1)S(1)}, u32[]{:S(2)}) copy-start(bf16[176,1536]{1,0:T(8,128)(2,1)S(1)} %get-tuple-element.28.refs_0_) | copy-start | bytes 1622020
  2.7 26.6 %collective-permute-start.4 = (bf16[96,1536]{1,0:T(8,128)(2,1)S(1)}, bf16[96,1536]{1,0:T(8,128)(2,1)S(1)}, u32[]{:S(2)}, u32[]{:S(2)}) collective-permute-start(bf16[96,1536]{1,0:T(8,128)(2,1)S(1)} %get-tuple-element.29), channel_id=1, source_target_pairs={{0,4},{2,6},{4,0},{6,2},{1,5},{3,7},{5,1},{7,3},{8,12},{10,14},{12... | collective-permute-start | bytes 884744 | tf_op jit(solution)/shard_map/ppermute | solution.py:289
  2.8 22.9 %collective-permute-start.12 = (bf16[80,1536]{1,0:T(8,128)(2,1)S(1)}, bf16[80,1536]{1,0:T(8,128)(2,1)}, u32[]{:S(2)}, u32[]{:S(2)}) collective-permute-start(bf16[80,1536]{1,0:T(8,128)(2,1)S(1)} %get-tuple-element.37), channel_id=1, source_target_pairs={{0,4},{2,6},{4,0},{6,2},{1,5},{3,7},{5,1},{7,3},{8,12},{10,14},{12... | collective-permute-start | bytes 737288 | tf_op jit(solution)/shard_map/ppermute | solution.py:289
  5.1 49.1 %collective-permute-start.5 = (bf16[176,1536]{1,0:T(8,128)(2,1)S(1)}, bf16[176,1536]{1,0:T(8,128)(2,1)S(1)}, u32[]{:S(2)}, u32[]{:S(2)}) collective-permute-start(bf16[176,1536]{1,0:T(8,128)(2,1)S(1)} %get-tuple-element.28.refs_0_), channel_id=1, source_target_pairs={{0,1},{1,0},{2,3},{3,2},{4,5},{5,4},{6,7},{7,6},{8,9},{9,8},{10,11... | collective-permute-start | bytes 1622024 | tf_op jit(solution)/shard_map/ppermute | solution.py:292
  6.4 49.1 %collective-permute-start.13 = (bf16[176,1536]{1,0:T(8,128)(2,1)S(1)}, bf16[176,1536]{1,0:T(8,128)(2,1)S(1)}, u32[]{:S(2)}, u32[]{:S(2)}) collective-permute-start(bf16[176,1536]{1,0:T(8,128)(2,1)S(1)} %get-tuple-element.38), channel_id=1, source_target_pairs={{0,2},{2,0},{4,6},{6,4},{1,3},{3,1},{5,7},{7,5},{8,10},{10,8},{12,... | collective-permute-start | bytes 1622024 | tf_op jit(solution)/shard_map/ppermute | solution.py:289
  7.7 46.3 %collective-permute-start = (bf16[96,1536]{1,0:T(8,128)(2,1)S(1)}, bf16[96,1536]{1,0:T(8,128)(2,1)S(1)}, u32[]{:S(2)}, u32[]{:S(2)}) collective-permute-start(bf16[96,1536]{1,0:T(8,128)(2,1)S(1)} %get-tuple-element.26), channel_id=1, source_target_pairs={{0,6},{2,4},{4,2},{6,0},{1,7},{3,5},{5,3},{7,1},{8,14},{10,12},{12... | collective-permute-start | bytes 884744 | tf_op jit(solution)/shard_map/ppermute | solution.py:289
  25.6 27.1 %collective-permute-start.1 = (bf16[80,1536]{1,0:T(8,128)(2,1)S(1)}, bf16[80,1536]{1,0:T(8,128)(2,1)}, u32[]{:S(2)}, u32[]{:S(2)}) collective-permute-start(bf16[80,1536]{1,0:T(8,128)(2,1)S(1)} %get-tuple-element.27), channel_id=1, source_target_pairs={{0,6},{2,4},{4,2},{6,0},{1,7},{3,5},{5,3},{7,1},{8,14},{10,12},{12... | collective-permute-start | bytes 737288 | tf_op jit(solution)/shard_map/ppermute | solution.py:289
  29.3 9.7 %copy-start.10 = (bf16[96,1536]{1,0:T(8,128)(2,1)}, bf16[96,1536]{1,0:T(8,128)(2,1)S(1)}, u32[]{:S(2)}) copy-start(bf16[96,1536]{1,0:T(8,128)(2,1)S(1)} %collective-permute-done.4.refs_1_) | copy-start | bytes 884740
  29.3 26.4 %collective-permute-start.6 = (bf16[96,1536]{1,0:T(8,128)(2,1)S(1)}, bf16[96,1536]{1,0:T(8,128)(2,1)S(1)}, u32[]{:S(2)}, u32[]{:S(2)}) collective-permute-start(bf16[96,1536]{1,0:T(8,128)(2,1)S(1)} %collective-permute-done.4.refs_1_), channel_id=1, source_target_pairs={{0,1},{1,0},{2,3},{3,2},{4,5},{5,4},{6,7},{7,6},{8,9},{9,8},{10,11... | collective-permute-start | bytes 884744 | tf_op jit(solution)/shard_map/ppermute | solution.py:292
  52.8 24.3 %collective-permute-start.14 = (bf16[80,1536]{1,0:T(8,128)(2,1)}, bf16[80,1536]{1,0:T(8,128)(2,1)S(1)}, u32[]{:S(2)}, u32[]{:S(2)}) collective-permute-start(bf16[80,1536]{1,0:T(8,128)(2,1)} %collective-permute-done.12.refs_0_), channel_id=1, source_target_pairs={{0,1},{1,0},{2,3},{3,2},{4,5},{5,4},{6,7},{7,6},{8,9},{9,8},{10,11... | collective-permute-start | bytes 737288 | tf_op jit(solution)/shard_map/ppermute | solution.py:292
  54.0 51.8 %copy-start.12 = (bf16[96,1536]{1,0:T(8,128)(2,1)}, bf16[96,1536]{1,0:T(8,128)(2,1)S(1)}, u32[]{:S(2)}) copy-start(bf16[96,1536]{1,0:T(8,128)(2,1)S(1)} %collective-permute-done.refs_0_) | copy-start | bytes 884740
  54.0 51.8 %collective-permute-start.3 = (bf16[80,1536]{1,0:T(8,128)(2,1)}, bf16[80,1536]{1,0:T(8,128)(2,1)}, u32[]{:S(2)}, u32[]{:S(2)}) collective-permute-start(bf16[80,1536]{1,0:T(8,128)(2,1)} %collective-permute-done.1.refs_1_), channel_id=1, source_target_pairs={{0,1},{1,0},{2,3},{3,2},{4,5},{5,4},{6,7},{7,6},{8,9},{9,8},{10,11... | collective-permute-start | bytes 737288 | tf_op jit(solution)/shard_map/ppermute | solution.py:292
  54.3 1.5 copy-start.7
  54.3 51.5 %collective-permute-start.2 = (bf16[96,1536]{1,0:T(8,128)(2,1)S(1)}, bf16[96,1536]{1,0:T(8,128)(2,1)S(1)}, u32[]{:S(2)}, u32[]{:S(2)}) collective-permute-start(bf16[96,1536]{1,0:T(8,128)(2,1)S(1)} %collective-permute-done.refs_0_), channel_id=1, source_target_pairs={{0,1},{1,0},{2,3},{3,2},{4,5},{5,4},{6,7},{7,6},{8,9},{9,8},{10,11... | collective-permute-start | bytes 884744 | tf_op jit(solution)/shard_map/ppermute | solution.py:292
  55.5 20.2 %copy-start.8 = (bf16[176,1536]{1,0:T(8,128)(2,1)}, bf16[176,1536]{1,0:T(8,128)(2,1)S(1)}, u32[]{:S(2)}) copy-start(bf16[176,1536]{1,0:T(8,128)(2,1)S(1)} %collective-permute-done.13.refs_1_) | copy-start | bytes 1622020
  55.5 27.7 %collective-permute-start.15 = (bf16[176,1536]{1,0:T(8,128)(2,1)S(1)}, bf16[176,1536]{1,0:T(8,128)(2,1)S(1)}, u32[]{:S(2)}, u32[]{:S(2)}) collective-permute-start(bf16[176,1536]{1,0:T(8,128)(2,1)S(1)} %collective-permute-done.13.refs_1_), channel_id=1, source_target_pairs={{0,1},{1,0},{2,3},{3,2},{4,5},{5,4},{6,7},{7,6},{8,9},{9,8},{10,11... | collective-permute-start | bytes 1622024 | tf_op jit(solution)/shard_map/ppermute | solution.py:292
  55.7 0.7 copy-start.11
  75.7 30.1 %copy-start = (bf16[49152,512]{1,0:T(8,128)(2,1)}, bf16[49152,512]{1,0:T(8,128)(2,1)S(1)}, u32[]{:S(2)}) copy-start(bf16[49152,512]{1,0:T(8,128)(2,1)S(1)} %get-tuple-element.30.refs_4_.refs_0_) | copy-start | bytes 150994944
  75.7 46.4 %collective-permute-start.18 = (bf16[96,1536]{1,0:T(8,128)(2,1)}, bf16[96,1536]{1,0:T(8,128)(2,1)S(1)}, u32[]{:S(2)}, u32[]{:S(2)}) collective-permute-start(bf16[96,1536]{1,0:T(8,128)(2,1)} %get-tuple-element.42), channel_id=1, source_target_pairs={{0,1},{1,0},{2,3},{3,2},{4,5},{5,4},{6,7},{7,6},{8,9},{9,8},{10,11... | collective-permute-start | bytes 884744 | tf_op jit(solution)/shard_map/ppermute | solution.py:292
  77.1 6.1 %copy-start.15 = (bf16[80,1536]{1,0:T(8,128)(2,1)}, bf16[80,1536]{1,0:T(8,128)(2,1)S(1)}, u32[]{:S(2)}) copy-start(bf16[80,1536]{1,0:T(8,128)(2,1)S(1)} %collective-permute-done.14.refs_2_) | copy-start | bytes 737284
  77.1 68.6 %collective-permute-start.11 = (bf16[176,1536]{1,0:T(8,128)(2,1)}, bf16[176,1536]{1,0:T(8,128)(2,1)S(1)}, u32[]{:S(2)}, u32[]{:S(2)}) collective-permute-start(bf16[176,1536]{1,0:T(8,128)(2,1)} %get-tuple-element.36), channel_id=1, source_target_pairs={{0,1},{1,0},{2,3},{3,2},{4,5},{5,4},{6,7},{7,6},{8,9},{9,8},{10,11... | collective-permute-start | bytes 1622024 | tf_op jit(solution)/shard_map/ppermute | solution.py:292
  83.2 1.9 %copy-start.9 = (bf16[176,1536]{1,0:T(8,128)(2,1)}, bf16[176,1536]{1,0:T(8,128)(2,1)S(1)}, u32[]{:S(2)}) copy-start(bf16[176,1536]{1,0:T(8,128)(2,1)S(1)} %collective-permute-done.15.refs_3_) | copy-start | bytes 1622020
  104.5 15.9 %copy-start.17 = (bf16[80,1536]{1,0:T(8,128)(2,1)S(1)}, bf16[80,1536]{1,0:T(8,128)(2,1)}, u32[]{:S(2)}) copy-start(bf16[80,1536]{1,0:T(8,128)(2,1)} %get-tuple-element.44) | copy-start | bytes 737284
  104.5 17.4 %copy-start.4 = (bf16[176,1536]{1,0:T(8,128)(2,1)S(1)}, bf16[176,1536]{1,0:T(8,128)(2,1)}, u32[]{:S(2)}) copy-start(bf16[176,1536]{1,0:T(8,128)(2,1)} %get-tuple-element.39.keep_ref) | copy-start | bytes 1622020
  104.5 17.4 %collective-permute-start.16 = (bf16[176,1536]{1,0:T(8,128)(2,1)}, bf16[176,1536]{1,0:T(8,128)(2,1)S(1)}, u32[]{:S(2)}, u32[]{:S(2)}) collective-permute-start(bf16[176,1536]{1,0:T(8,128)(2,1)} %get-tuple-element.40), channel_id=1, source_target_pairs={{0,1},{1,0},{2,3},{3,2},{4,5},{5,4},{6,7},{7,6},{8,9},{9,8},{10,11... | collective-permute-start | bytes 1622024 | tf_op jit(solution)/shard_map/ppermute | solution.py:292
  105.8 0.7 copy-start.14
  120.5 19.7 %collective-permute-start.20 = (bf16[80,1536]{1,0:T(8,128)(2,1)S(1)}, bf16[80,1536]{1,0:T(8,128)(2,1)S(1)}, u32[]{:S(2)}, u32[]{:S(2)}) collective-permute-start(bf16[80,1536]{1,0:T(8,128)(2,1)S(1)} %copy-done.17), channel_id=1, source_target_pairs={{0,1},{1,0},{2,3},{3,2},{4,5},{5,4},{6,7},{7,6},{8,9},{9,8},{10,11... | collective-permute-start | bytes 737288 | tf_op jit(solution)/shard_map/ppermute | solution.py:292
  120.7 22.1 %collective-permute-start.7 = (bf16[96,1536]{1,0:T(8,128)(2,1)}, bf16[96,1536]{1,0:T(8,128)(2,1)S(1)}, u32[]{:S(2)}, u32[]{:S(2)}) collective-permute-start(bf16[96,1536]{1,0:T(8,128)(2,1)} %get-tuple-element.32), channel_id=1, source_target_pairs={{0,1},{1,0},{2,3},{3,2},{4,5},{5,4},{6,7},{7,6},{8,9},{9,8},{10,11... | collective-permute-start | bytes 884744 | tf_op jit(solution)/shard_map/ppermute | solution.py:292
  122.1 54.1 %collective-permute-start.17 = (bf16[176,1536]{1,0:T(8,128)(2,1)S(1)}, bf16[176,1536]{1,0:T(8,128)(2,1)S(1)}, u32[]{:S(2)}, u32[]{:S(2)}) collective-permute-start(bf16[176,1536]{1,0:T(8,128)(2,1)S(1)} %shard_map.63), channel_id=1, source_target_pairs={{0,2},{2,0},{4,6},{6,4},{1,3},{3,1},{5,7},{7,5},{8,10},{10,8},{12,... | collective-permute-start | bytes 1622024 | tf_op jit(solution)/shard_map/ppermute | solution.py:289
  122.2 0.7 copy-start.13
  122.2 22.4 %collective-permute-start.9 = (bf16[80,1536]{1,0:T(8,128)(2,1)}, bf16[80,1536]{1,0:T(8,128)(2,1)S(1)}, u32[]{:S(2)}, u32[]{:S(2)}) collective-permute-start(bf16[80,1536]{1,0:T(8,128)(2,1)} %get-tuple-element.34), channel_id=1, source_target_pairs={{0,1},{1,0},{2,3},{3,2},{4,5},{5,4},{6,7},{7,6},{8,9},{9,8},{10,11... | collective-permute-start | bytes 737288 | tf_op jit(solution)/shard_map/ppermute | solution.py:292
  122.9 15.5 %copy-start.1 = (bf16[49152,512]{1,0:T(8,128)(2,1)S(1)}, bf16[49152,512]{1,0:T(8,128)(2,1)}, u32[]{:S(2)}) copy-start(bf16[49152,512]{1,0:T(8,128)(2,1)} %copy-done) | copy-start | bytes 150994944
  140.2 0.7 copy-start.16
  140.2 29.7 %collective-permute-start.19 = (bf16[96,1536]{1,0:T(8,128)(2,1)}, bf16[96,1536]{1,0:T(8,128)(2,1)S(1)}, u32[]{:S(2)}, u32[]{:S(2)}) collective-permute-start(bf16[96,1536]{1,0:T(8,128)(2,1)} %shard_map.64), channel_id=1, source_target_pairs={{0,4},{2,6},{4,0},{6,2},{1,5},{3,7},{5,1},{7,3},{8,12},{10,14},{12... | collective-permute-start | bytes 884744 | tf_op jit(solution)/shard_map/ppermute | solution.py:289
  140.9 3.6 %copy-start.5 = (bf16[96,1536]{1,0:T(8,128)(2,1)S(1)}, bf16[96,1536]{1,0:T(8,128)(2,1)}, u32[]{:S(2)}) copy-start(bf16[96,1536]{1,0:T(8,128)(2,1)} %get-tuple-element.31.keep_ref) | copy-start | bytes 884740
  140.9 4.7 %copy-start.6 = (bf16[80,1536]{1,0:T(8,128)(2,1)S(1)}, bf16[80,1536]{1,0:T(8,128)(2,1)}, u32[]{:S(2)}) copy-start(bf16[80,1536]{1,0:T(8,128)(2,1)} %get-tuple-element.33.keep_ref) | copy-start | bytes 737284
  140.9 5.4 %copy-start.3 = (bf16[176,1536]{1,0:T(8,128)(2,1)S(1)}, bf16[176,1536]{1,0:T(8,128)(2,1)}, u32[]{:S(2)}) copy-start(bf16[176,1536]{1,0:T(8,128)(2,1)} %get-tuple-element.35.keep_ref) | copy-start | bytes 1622020
  142.8 32.3 %collective-permute-start.21 = (bf16[80,1536]{1,0:T(8,128)(2,1)}, bf16[80,1536]{1,0:T(8,128)(2,1)S(1)}, u32[]{:S(2)}, u32[]{:S(2)}) collective-permute-start(bf16[80,1536]{1,0:T(8,128)(2,1)} %shard_map.65), channel_id=1, source_target_pairs={{0,4},{2,6},{4,0},{6,2},{1,5},{3,7},{5,1},{7,3},{8,12},{10,14},{12... | collective-permute-start | bytes 737288 | tf_op jit(solution)/shard_map/ppermute | solution.py:289
  144.6 45.7 %collective-permute-start.8 = (bf16[96,1536]{1,0:T(8,128)(2,1)S(1)}, bf16[96,1536]{1,0:T(8,128)(2,1)S(1)}, u32[]{:S(2)}, u32[]{:S(2)}) collective-permute-start(bf16[96,1536]{1,0:T(8,128)(2,1)S(1)} %shard_map.59), channel_id=1, source_target_pairs={{0,6},{2,4},{4,2},{6,0},{1,7},{3,5},{5,3},{7,1},{8,14},{10,12},{12... | collective-permute-start | bytes 884744 | tf_op jit(solution)/shard_map/ppermute | solution.py:289
  145.7 44.6 %collective-permute-start.10 = (bf16[80,1536]{1,0:T(8,128)(2,1)S(1)}, bf16[80,1536]{1,0:T(8,128)(2,1)S(1)}, u32[]{:S(2)}, u32[]{:S(2)}) collective-permute-start(bf16[80,1536]{1,0:T(8,128)(2,1)S(1)} %shard_map.60), channel_id=1, source_target_pairs={{0,6},{2,4},{4,2},{6,0},{1,7},{3,5},{5,3},{7,1},{8,14},{10,12},{12... | collective-permute-start | bytes 737288 | tf_op jit(solution)/shard_map/ppermute | solution.py:289
